TPU v7x, 16 devices: a 4x2x1 block of a 4x4x8 slice. The times are simulated.
16 devices in a mesh: data: 2 (over y, z), seq: 8 (over x, core).
Axes of the slice: x: 4, y: 2, z: 1, core: 2. Of those that a mesh axis runs over, the one named last changes fastest.
The devices are a block of a 4x4x8 slice.
Arguments:
- x_tok: bfloat16 [32768, 768], P(('data', 'seq')), parts along dimension 0
- dy_tok: bfloat16 [32768, 768], P(('data', 'seq')), parts along dimension 0
- ln_gamma: float32 [768], replicated
- ln_beta: float32 [768], replicated
- w_qkv: bfloat16 [768, 3, 16, 48], replicated
- w_out: bfloat16 [768, 768], replicated
Outputs:
- output 1: bfloat16 [32768, 768], P(('data', 'seq')), parts along dimension 0
- output 2: bfloat16 [32768, 768], P(('data', 'seq')), parts along dimension 0
- output 3: float32 [1536, 3, 16, 48], P(('data', 'seq')), parts along dimension 0
- output 4: float32 [1536, 768], P(('data', 'seq')), parts along dimension 0
- output 5: float32 [1536], P('data'), parts along dimension 0
- output 6: float32 [1536], P('data'), parts along dimension 0
There are 2 independent parts. A program takes and returns all parts, laid end to end along the dimension named above; an argument that names none is the same for every part.
All inputs are finite; a program needn't handle non-finite values.
Results may differ from a plain program's by a relative error of at most 0.00480294.
Values are sent between devices in bfloat16 or wider.
A program may use at most 768 MiB of HBM per device.

v0:
```python
import functools

import jax
import jax.numpy as jnp
from jax import lax
from jax.experimental import pallas as pl
from jax.experimental.pallas import tpu as pltpu
from jax.sharding import PartitionSpec as P

LN_EPS = 1e-5
MESH = pl.DeviceIdType.MESH
F32 = jnp.float32
BF16 = jnp.bfloat16
TT = 512
BLK = 256


def nn(a, b):
    return lax.dot_general(a, b, (((1,), (0,)), ((), ())), preferred_element_type=F32)


def nt(a, b):
    return lax.dot_general(a, b, (((1,), (1,)), ((), ())), preferred_element_type=F32)


def kernel(n, heads, hd,
           x_hbm, dy_hbm, gam_ref, bet_ref, wt_hbm, wo_hbm,
           y_hbm, dx_hbm, dwqkv_ref, dwo_ref, dg_ref, db_ref,
           xbuf, dybuf, wt, wo, w, wot, xT, dyT, uT, qkvT, oT, mean_ref, rstd_ref, gb, bb,
           s_acc, comp, ar_in, ar_out, sx, sg, sgt, zb, dzacc,
           acc, d2d, relay, fin, dgacc, dbacc, dgslots,
           sem_in, sem_out, ar_send, ar_recv, rs_send, rs_recv, dg_send, dg_recv):
    tokens, width = xbuf.shape
    steps = tokens // TT
    groups = 4
    hpg = heads // groups
    gr = hpg * hd
    nb = width // BLK
    chips = n // 2
    me = lax.axis_index("seq")
    chip, core = lax.div(me, 2), lax.rem(me, 2)
    partner = 2 * chip + (1 - core)
    c_right, c_left = lax.rem(chip + 1, chips), lax.rem(chip + chips - 1, chips)
    c_opp = lax.rem(chip + 2, chips)
    right, left = 2 * c_right + core, 2 * c_left + core

    def x_copy(t):
        r = pl.ds(pl.multiple_of(t * TT, TT), TT)
        return pltpu.make_async_copy(x_hbm.at[r, :], xbuf.at[r, :], sem_in.at[0, t])

    def dy_copy(t):
        r = pl.ds(pl.multiple_of(t * TT, TT), TT)
        return pltpu.make_async_copy(dy_hbm.at[r, :], dybuf.at[r, :], sem_in.at[1, t])

    wkv_copy = pltpu.make_async_copy(wt_hbm.at[pl.ds(width, 2 * width), :], wt.at[pl.ds(width, 2 * width), :], sem_in.at[2, 0])
    wq_copy = pltpu.make_async_copy(wt_hbm.at[pl.ds(0, width), :], wt.at[pl.ds(0, width), :], sem_in.at[2, 1])
    wo_copy = pltpu.make_async_copy(wo_hbm, wo, sem_in.at[2, 2])
    x_copy(0).start()
    wkv_copy.start()
    for t in range(1, steps):
        x_copy(t).start()
    for t in range(steps):
        dy_copy(t).start()
    wq_copy.start()
    wo_copy.start()

    barrier = pltpu.get_barrier_semaphore()
    for d in range(1, n):
        pl.semaphore_signal(barrier, inc=1, device_id={"seq": lax.rem(me + d, n)}, device_id_type=MESH)

    eye = (lax.broadcasted_iota(jnp.int32, (BLK, BLK), 0) == lax.broadcasted_iota(jnp.int32, (BLK, BLK), 1)).astype(F32).astype(BF16)
    gb[...] = jnp.transpose(jnp.broadcast_to(gam_ref[...], (128, width)))
    bb[...] = jnp.transpose(jnp.broadcast_to(bet_ref[...], (128, width)))
    s_acc[...] = jnp.zeros_like(s_acc)
    sx[...] = jnp.zeros_like(sx)
    dzacc[...] = jnp.zeros_like(dzacc)
    dgacc[...] = jnp.zeros_like(dgacc)
    dbacc[...] = jnp.zeros_like(dbacc)

    def lanes(ref_val):
        return jnp.concatenate([ref_val] * (TT // 128), axis=1)

    def fold(v):
        out = v[:, :128]
        for i in range(1, TT // 128):
            out = out + v[:, 128 * i:128 * (i + 1)]
        return out

    def tok(t):
        return pl.ds(pl.multiple_of(t * TT, TT), TT)

    wkv_copy.wait()

    @pl.loop(0, steps)
    def _(t):
        ts = tok(t)
        x_copy(t).wait()
        xt = jnp.concatenate([nt(eye, xbuf[ts, BLK * b:BLK * (b + 1)]) for b in range(nb)], axis=0)
        xT[:, ts] = xt.astype(BF16)
        mean = jnp.sum(xt, axis=0, keepdims=True) * (1.0 / width)
        cen = xt - mean
        var = jnp.sum(cen * cen, axis=0, keepdims=True) * (1.0 / width)
        rstd = lax.rsqrt(var + LN_EPS)
        mean_ref[:, ts] = mean
        rstd_ref[:, ts] = rstd
        uT[:, ts] = (cen * rstd * lanes(gb[...]) + lanes(bb[...])).astype(BF16)
        for g in range(groups):
            ks, vs = width + gr * g, 2 * width + gr * g
            kb = nn(wt[ks:ks + gr, :], uT[:, ts]).astype(BF16)
            vb = nn(wt[vs:vs + gr, :], uT[:, ts]).astype(BF16)
            qkvT[ks:ks + gr, ts] = kb
            qkvT[vs:vs + gr, ts] = vb
            k32 = kb.astype(F32)
            fk = jnp.where(k32 > 0, k32 + 1.0, jnp.exp(jnp.minimum(k32, 0.0))).astype(BF16)
            ve = jnp.concatenate([vb, jnp.ones((BLK - gr, TT), BF16)], axis=0)
            s_acc[g] += nt(fk, ve)

    lane128 = lax.broadcasted_iota(jnp.int32, (hd, 128), 1)
    lane256 = lax.broadcasted_iota(jnp.int32, (hd, BLK), 1)
    half_heads = heads // 2

    def compact(z_of):
        def head(h):
            g, hh = h // hpg, h % hpg
            blk = s_acc[g, hd * hh:hd * (hh + 1), :]
            moved = pltpu.roll(blk, BLK - hd * hh, axis=1) if hh else blk
            return jnp.where(lane128 < hd, moved[:, :128], jnp.where(lane128 == hd, z_of(h, blk), 0.0))

        for p in range(half_heads):
            comp[p] = head(p) + pltpu.roll(head(p + half_heads), 64, axis=1)

    def ar1(i, d):
        peer = lax.rem(me + d, n)
        return pltpu.make_async_remote_copy(
            src_ref=comp.at[peer], dst_ref=ar_in.at[i, d], send_sem=ar_send.at[2 * i, d], recv_sem=ar_recv.at[2 * i, d],
            device_id={"seq": peer}, device_id_type=MESH)

    def ar2(i, d):
        peer = lax.rem(me + d, n)
        return pltpu.make_async_remote_copy(
            src_ref=ar_out.at[i, 0], dst_ref=ar_out.at[i, d], send_sem=ar_send.at[2 * i + 1, d], recv_sem=ar_recv.at[2 * i + 1, d],
            device_id={"seq": peer}, device_id_type=MESH)

    def ar_reduce(i):
        total = comp[me]
        for d in range(1, n):
            ar1(i, d).wait_recv()
            total = total + ar_in[i, d]
        ar_out[i, 0] = total
        for d in range(1, n):
            ar1(i, d).wait_send()
        for d in range(1, n):
            ar2(i, d).start()

    def ar_finish(i, z_round, with_z):
        for d in range(1, n):
            ar2(i, d).wait_recv()
        for p in range(half_heads):
            piece = ar_out[i, lax.rem(me - p + n, n)]
            for h, part in ((p, piece), (p + half_heads, pltpu.roll(piece, 64, axis=1))):
                g, hh = h // hpg, h % hpg
                zc = part[:, hd:hd + 1]
                if z_round:
                    zc = zc.astype(BF16).astype(F32)
                blk = jnp.where(lane128 < hd, part, 0.0)
                wide = jnp.concatenate([blk, jnp.zeros((hd, 128), F32)], axis=1)
                if hh:
                    wide = pltpu.roll(wide, hd * hh, axis=1)
                if with_z:
                    wide = jnp.where(lane256 == gr + hh, jnp.broadcast_to(zc, (hd, BLK)), wide)
                sx[g, hd * hh:hd * (hh + 1), :] = wide
                zb[hd * h:hd * (h + 1), :] = jnp.broadcast_to(zc, (hd, 128))
        for g in range(groups):
            m = sx[g]
            sg[g] = m[:gr, :gr].astype(BF16)
            sgt[g] = jnp.transpose(m)[:sgt.shape[1], :gr].astype(BF16)

    compact(lambda h, blk: blk[:, gr:gr + 1])
    pl.semaphore_wait(barrier, n - 1)
    for d in range(1, n):
        ar1(0, d).start()

    wq_copy.wait()

    @pl.loop(0, steps)
    def _(t):
        ts = tok(t)
        dy_copy(t).wait()
        for b in range(nb):
            dyT[BLK * b:BLK * (b + 1), ts] = nt(eye, dybuf[ts, BLK * b:BLK * (b + 1)]).astype(BF16)
        qkvT[0:width, ts] = nn(wt[0:width, :], uT[:, ts]).astype(BF16)

    ar_reduce(0)
    wo_copy.wait()
    for i in range(nb):
        for j in range(nb):
            wot[BLK * j:BLK * (j + 1), BLK * i:BLK * (i + 1)] = nt(eye, wo[BLK * i:BLK * (i + 1), BLK * j:BLK * (j + 1)]).astype(BF16)

    @pl.loop(0, 3 * nb)
    def _(j):
        js = pl.ds(pl.multiple_of(j * BLK, BLK), BLK)
        for i in range(nb):
            w[BLK * i:BLK * (i + 1), js] = nt(eye, wt[js, BLK * i:BLK * (i + 1)]).astype(BF16)

    ar_finish(0, True, True)
    s_acc[...] = jnp.zeros_like(s_acc)

    def per_head(v):
        return jnp.broadcast_to(v[:, None, :], (hpg, hd, TT)).reshape(gr, TT)

    @pl.loop(0, steps)
    def _(t):
        ts = tok(t)
        for g in range(groups):
            rows = slice(gr * g, gr * (g + 1))
            q32 = qkvT[rows, ts].astype(F32)
            ex = jnp.exp(jnp.minimum(q32, 0.0))
            fq = jnp.where(q32 > 0, q32 + 1.0, ex).astype(BF16)
            slope = jnp.where(q32 > 0, 1.0, ex)
            nd = nn(sgt[g], fq)
            rden = per_head(1.0 / nd[gr:gr + hpg])
            a = nd[:gr] * rden
            oT[rows, ts] = a.astype(BF16)
            gg = (nn(wo[rows, :], dyT[:, ts]) * rden).astype(BF16)
            c = jnp.sum((gg.astype(F32) * a).reshape(hpg, hd, TT), axis=1)
            cb = per_head(c)
            dfq = nn(sg[g], gg) - cb * lanes(zb[rows, :])
            qkvT[rows, ts] = (dfq * slope).astype(BF16)
            ge = jnp.concatenate([gg, jnp.zeros((BLK - gr, TT), BF16)], axis=0)
            s_acc[g] += nt(fq, ge)
            dzacc[rows, :] -= fold(cb * fq.astype(F32))

    compact(lambda h, blk: jnp.sum(dzacc[hd * h:hd * (h + 1), :], axis=1, keepdims=True))
    for d in range(1, n):
        ar1(1, d).start()

    half_rows = width // 2

    def grad_wo():
        @pl.loop(0, 2)
        def _(m):
            rs = pl.ds(pl.multiple_of(m * half_rows, half_rows), half_rows)
            out = nn(oT[rs, :], dybuf[...])
            acc[0, pl.ds(2 * m, 2)] = out.reshape(2, 2, width // n, width)

    def grad_w(j):
        @pl.loop(0, 2)
        def _(m):
            rs = pl.ds(pl.multiple_of(m * half_rows, half_rows), half_rows)
            out = nt(uT[rs, :], qkvT[width * (j - 1):width * j, :])
            acc[j, pl.ds(2 * m, 2)] = out.reshape(2, 2, width // n, width)

    hr = width // n // 2
    lo, hi = pl.ds(0, hr), pl.ds(hr, hr)

    def rdma(u, s, src, dst, peer):
        return pltpu.make_async_remote_copy(src_ref=src, dst_ref=dst, send_sem=rs_send.at[u, s], recv_sem=rs_recv.at[u, s],
                                            device_id={"seq": peer}, device_id_type=MESH)

    def d2d_copy(u, c):
        return rdma(u, c, acc.at[u, c, 1 - core], d2d.at[u, c], partner)

    def hop(u, s):
        if s == 0:
            return rdma(u, chips, acc.at[u, c_opp, core, lo], relay.at[u, 0], right)
        if s == 1:
            return rdma(u, chips + 1, acc.at[u, c_opp, core, hi], relay.at[u, 1], left)
        if s == 2:
            return rdma(u, chips + 2, acc.at[u, c_right, core, hi], fin.at[u, 0, hi], right)
        if s == 3:
            return rdma(u, chips + 3, acc.at[u, c_left, core, lo], fin.at[u, 1, lo], left)
        if s == 4:
            return rdma(u, chips + 4, acc.at[u, c_right, core, lo], fin.at[u, 0, lo], right)
        return rdma(u, chips + 5, acc.at[u, c_left, core, hi], fin.at[u, 1, hi], left)

    def rs_pair(u):
        for c in range(chips):
            d2d_copy(u, c).start()

    def rs_chip(u):
        for c in range(chips):
            d2d_copy(u, c).wait_recv()
        acc[u, c_opp, core] += d2d[u, c_opp]
        hop(u, 0).start()
        hop(u, 1).start()
        acc[u, c_right, core] += d2d[u, c_right]
        hop(u, 2).start()
        acc[u, c_left, core] += d2d[u, c_left]
        hop(u, 3).start()
        acc[u, chip, core] += d2d[u, chip]

    def rs_relay(u):
        hop(u, 0).wait_recv()
        acc[u, c_right, core, lo] += relay[u, 0]
        hop(u, 4).start()
        hop(u, 1).wait_recv()
        acc[u, c_left, core, hi] += relay[u, 1]
        hop(u, 5).start()

    def rs_final(u, out_ref, cols):
        for s in range(2, 6):
            hop(u, s).wait_recv()
        out_ref[:, cols] = acc[u, chip, core] + fin[u, 0] + fin[u, 1]

    grad_wo()
    rs_pair(0)
    ar_reduce(1)
    grad_w(1)
    rs_pair(1)
    rs_chip(0)
    ar_finish(1, False, False)

    @pl.loop(0, steps)
    def _(t):
        ts = tok(t)
        for g in range(groups):
            kr = slice(width + gr * g, width + gr * (g + 1))
            vr = slice(2 * width + gr * g, 2 * width + gr * (g + 1))
            k32 = qkvT[kr, ts].astype(F32)
            ex = jnp.exp(jnp.minimum(k32, 0.0))
            fk = jnp.where(k32 > 0, k32 + 1.0, ex).astype(BF16)
            slope = jnp.where(k32 > 0, 1.0, ex)
            dfk = nn(sg[g], qkvT[vr, ts]) + lanes(zb[gr * g:gr * (g + 1), :])
            qkvT[kr, ts] = (dfk * slope).astype(BF16)
            qkvT[vr, ts] = nn(sgt[g, :gr, :], fk).astype(BF16)

    rs_chip(1)
    grad_w(2)
    rs_pair(2)
    rs_relay(0)
    grad_w(3)
    rs_pair(3)
    rs_chip(2)
    rs_relay(1)

    def y_copy(t):
        r = tok(t)
        return pltpu.make_async_copy(xbuf.at[r, :], y_hbm.at[r, :], sem_out.at[0, t])

    def dx_copy(t):
        r = tok(t)
        return pltpu.make_async_copy(dybuf.at[r, :], dx_hbm.at[r, :], sem_out.at[1, t])

    def store_tokens(buf, t, val):
        for s in range(TT // BLK):
            r = pl.ds(pl.multiple_of(t * TT + BLK * s, BLK), BLK)
            for b in range(nb):
                buf[r, BLK * b:BLK * (b + 1)] = nt(eye, val[BLK * b:BLK * (b + 1), BLK * s:BLK * (s + 1)]).astype(BF16)

    @pl.loop(0, steps)
    def _(t):
        ts = tok(t)
        yt = (nn(wot[...], oT[:, ts]) + xT[:, ts].astype(F32)).astype(BF16)
        store_tokens(xbuf, t, yt)
        y_copy(t).start()

    rs_chip(3)

    @pl.loop(0, steps)
    def _(t):
        ts = tok(t)
        du = nn(w[...], qkvT[:, ts])
        rstd = rstd_ref[:, ts]
        xhat = (xT[:, ts].astype(F32) - mean_ref[:, ts]) * rstd
        dgacc[...] += fold(du * xhat)
        dbacc[...] += fold(du)
        e = du * lanes(gb[...])
        m1 = jnp.sum(e, axis=0, keepdims=True) * (1.0 / width)
        m2 = jnp.sum(e * xhat, axis=0, keepdims=True) * (1.0 / width)
        dxt = (dyT[:, ts].astype(F32) + rstd * (e - m1 - xhat * m2)).astype(BF16)
        store_tokens(dybuf, t, dxt)
        dx_copy(t).start()

    def dg_copy(d):
        return pltpu.make_async_remote_copy(
            src_ref=dgslots.at[0], dst_ref=dgslots.at[d], send_sem=dg_send.at[d], recv_sem=dg_recv.at[d],
            device_id={"seq": lax.rem(me + d, n)}, device_id_type=MESH)

    dgrow = jnp.sum(jnp.transpose(dgacc[...]), axis=0, keepdims=True)
    dbrow = jnp.sum(jnp.transpose(dbacc[...]), axis=0, keepdims=True)
    sub = lax.broadcasted_iota(jnp.int32, (8, width), 0)
    dgslots[0] = jnp.where(sub == 0, dgrow, jnp.where(sub == 1, dbrow, 0.0))
    for d in range(1, n):
        dg_copy(d).start()

    rs_relay(2)
    rs_relay(3)
    rs_final(0, dwo_ref, slice(0, width))
    for u in range(1, 4):
        rs_final(u, dwqkv_ref, slice(width * (u - 1), width * u))

    for d in range(1, n):
        dg_copy(d).wait_recv()
    total = dgslots[lax.rem(me, n)]
    for p in range(1, n):
        total = total + dgslots[lax.rem(me - p + n, n)]
    dg_ref[...] = total[0:1]
    db_ref[...] = total[1:2]

    for d in range(1, n):
        ar2(0, d).wait_send()
        ar2(1, d).wait_send()
        dg_copy(d).wait_send()
    for u in range(4):
        for c in range(chips):
            d2d_copy(u, c).wait_send()
        for s in range(6):
            hop(u, s).wait_send()

    @pl.loop(0, steps)
    def _(t):
        y_copy(t).wait()
        dx_copy(t).wait()


def local_block(n, x_tok, dy_tok, ln_gamma, ln_beta, w_qkv, w_out):
    tokens, width = x_tok.shape
    _, three, heads, hd = w_qkv.shape
    wt = w_qkv.transpose(1, 2, 3, 0).reshape(three * width, width)
    steps = tokens // TT
    chips = n // 2
    own = width // n
    hbm = pl.BlockSpec(memory_space=pl.ANY)
    vmem = pl.BlockSpec(memory_space=pltpu.VMEM)
    gr = heads * hd // 4
    dma = pltpu.SemaphoreType.DMA
    y, dx, dwqkv, dwo, dg, db = pl.pallas_call(
        functools.partial(kernel, n, heads, hd),
        name="block",
        out_shape=(
            jax.ShapeDtypeStruct((tokens, width), BF16), jax.ShapeDtypeStruct((tokens, width), BF16),
            jax.ShapeDtypeStruct((own, three * width), F32), jax.ShapeDtypeStruct((own, width), F32),
            jax.ShapeDtypeStruct((1, width), F32), jax.ShapeDtypeStruct((1, width), F32)),
        in_specs=[hbm, hbm, vmem, vmem, hbm, hbm],
        out_specs=(hbm, hbm, vmem, vmem, vmem, vmem),
        scratch_shapes=[
            pltpu.VMEM((tokens, width), BF16), pltpu.VMEM((tokens, width), BF16),
            pltpu.VMEM((three * width, width), BF16), pltpu.VMEM((width, width), BF16),
            pltpu.VMEM((width, three * width), BF16), pltpu.VMEM((width, width), BF16),
            pltpu.VMEM((width, tokens), BF16), pltpu.VMEM((width, tokens), BF16), pltpu.VMEM((width, tokens), BF16),
            pltpu.VMEM((three * width, tokens), BF16), pltpu.VMEM((width, tokens), BF16),
            pltpu.VMEM((1, tokens), F32), pltpu.VMEM((1, tokens), F32),
            pltpu.VMEM((width, 128), F32), pltpu.VMEM((width, 128), F32),
            pltpu.VMEM((4, gr, BLK), F32), pltpu.VMEM((heads // 2, hd, 128), F32),
            pltpu.VMEM((2, n, hd, 128), F32), pltpu.VMEM((2, n, hd, 128), F32),
            pltpu.VMEM((4, BLK, BLK), F32), pltpu.VMEM((4, gr, gr), BF16), pltpu.VMEM((4, gr + 16, gr), BF16),
            pltpu.VMEM((width, 128), F32), pltpu.VMEM((width, 128), F32),
            pltpu.VMEM((4, chips, 2, own, width), F32), pltpu.VMEM((4, chips, own, width), F32),
            pltpu.VMEM((4, 2, own // 2, width), F32), pltpu.VMEM((4, 2, own, width), F32),
            pltpu.VMEM((width, 128), F32), pltpu.VMEM((width, 128), F32), pltpu.VMEM((n, 8, width), F32),
            dma((3, max(steps, 3))), dma((2, steps)),
            dma((4, n)), dma((4, n)), dma((4, chips + 6)), dma((4, chips + 6)), dma((n,)), dma((n,)),
        ],
        compiler_params=pltpu.CompilerParams(collective_id=0, has_side_effects=True, vmem_limit_bytes=67_000_000),
    )(x_tok, dy_tok, ln_gamma.reshape(1, width), ln_beta.reshape(1, width), wt, w_out)
    return y, dx, dwqkv.reshape(own, three, heads, hd), dwo, dg.reshape(width), db.reshape(width)


def solution(mesh):
    rows = P(("data", "seq"), None)
    return jax.shard_map(
        functools.partial(local_block, mesh.shape["seq"]), mesh=mesh,
        in_specs=(rows, rows, P(None), P(None), P(None, None, None, None), P(None, None)),
        out_specs=(rows, rows, P(("data", "seq"), None, None, None), rows, P("data"), P("data")),
        check_vma=False)
```

profile of v0, /device:TPU:113, one launch (start us, length us, event | category | flops | bytes accessed | tf_op | source)
XLA Modules:
  0.0 106.7 jit_solution(15994834601653970298)
XLA Ops:
  0.6 1.3 %reshape.30.gam_ref = f32[1,768]{1,0:T(1,128)} reshape(f32[768]{0:T(1024)} %param.8) | data formatting | bytes 6144 | tf_op jit(solution)/shard_map/reshape | solution.py:455
  1.9 1.3 %reshape.31.bet_ref = f32[1,768]{1,0:T(1,128)} reshape(f32[768]{0:T(1024)} %param.9) | data formatting | bytes 6144 | tf_op jit(solution)/shard_map/reshape | solution.py:455
  3.2 92.1 %block.1 = (bf16[2048,768]{1,0:T(8,128)(2,1)}, bf16[2048,768]{1,0:T(8,128)(2,1)}, f32[96,2304]{1,0:T(8,128)}, f32[96,768]{1,0:T(8,128)}, f32[1,768]{1,0:T(1,128)}, /*index=5*/f32[1,768]{1,0:T(1,128)}) custom-call(bf16[2048,768]{1,0:T(8,128)(2,1)} %x_hbm.1, bf16[2048,768]{1,0:T(8,128)(2,1)} %dy_hbm.1, f32[1,768]{1,0:T(1,128)} %reshape.30.gam_ref, ...), custom_call_target="tpu_custom_call" | custom-call | tf_op jit(solution)/shard_map/block/pallas_call | solution.py:427
  95.3 2.6 %copy.13 = f32[96,2304]{0,1:T(8,128)} copy(f32[96,2304]{1,0:T(8,128)} %get-tuple-element.14) | data formatting | bytes 1769472 | tf_op jit(solution)/shard_map/block/pallas_call | solution.py:427
  97.8 1.3 %reduce = f32[768]{0:T(1024)} reduce(f32[1,768]{1,0:T(1,128)} %get-tuple-element.16, f32[]{:T(128)} %constant), dimensions={0}, to_apply=%get-tuple-element.16.reduce_sub_computation | reduce | bytes 6148 | tf_op jit(solution)/shard_map/block/pallas_call | solution.py:427
  99.1 1.3 %reduce.1 = f32[768]{0:T(1024)} reduce(f32[1,768]{1,0:T(1,128)} %get-tuple-element.17, f32[]{:T(128)} %constant), dimensions={0}, to_apply=%get-tuple-element.17.reduce_sub_computation | reduce | bytes 6148 | tf_op jit(solution)/shard_map/block/pallas_call | solution.py:427
  100.4 0.0 copy-start
  100.4 3.9 %copy.17 = bf16[2048,768]{1,0:T(8,128)(2,1)} copy(bf16[2048,768]{1,0:T(8,128)(2,1)} %get-tuple-element.30) | data formatting | bytes 6291456
  104.3 0.0 copy-done
  104.3 0.0 copy-start.1
  104.3 1.7 %copy.18 = bf16[2048,768]{1,0:T(8,128)(2,1)} copy(bf16[2048,768]{1,0:T(8,128)(2,1)S(1)} %copy-done) | data formatting | bytes 6291456
  106.0 0.0 copy-done.1
  106.0 0.7 copy.19
Async XLA Ops:
  100.4 3.9 %copy-start = (bf16[2048,768]{1,0:T(8,128)(2,1)S(1)}, bf16[2048,768]{1,0:T(8,128)(2,1)}, u32[]{:S(2)}) copy-start(bf16[2048,768]{1,0:T(8,128)(2,1)} %get-tuple-element.31) | copy-start | bytes 9437188
  104.3 1.7 %copy-start.1 = (f32[96,768]{1,0:T(8,128)S(1)}, f32[96,768]{1,0:T(8,128)}, u32[]{:S(2)}) copy-start(f32[96,768]{1,0:T(8,128)} %get-tuple-element.33) | copy-start | bytes 884740
where the time goes:
time: 107 us
  Pallas kernels  92.1 us (86%)
  local copies, waits for them, and re-layouts  11.4 us (11%)
  other arithmetic  2.55 us (2%)
    pallas_call x1, Pallas kernels, local_block(): pl.pallas_call(functools.partial(kernel, n, heads, hd), name='block', out...  92.1 us
    unnamed x7, local copies, waits for them, and re-layouts  6.29 us
    pallas_call x1, local copies, waits for them, and re-layouts, local_block(): pl.pallas_call(functools.partial(kernel, n, heads, hd), name='block', out...  2.55 us
    pallas_call x2, other arithmetic, local_block(): pl.pallas_call(functools.partial(kernel, n, heads, hd), name='block', out...  2.55 us

commit v1 on v0

v1 whole, which is shorter than its diff:
```python
import functools

import jax
import jax.numpy as jnp
from jax import lax
from jax.experimental import pallas as pl
from jax.experimental.pallas import tpu as pltpu
from jax.sharding import PartitionSpec as P

LN_EPS = 1e-5
MESH = pl.DeviceIdType.MESH
F32 = jnp.float32
BF16 = jnp.bfloat16
TT = 512
BLK = 256


def nn(a, b):
    return lax.dot_general(a, b, (((1,), (0,)), ((), ())), preferred_element_type=F32)


def nt(a, b):
    return lax.dot_general(a, b, (((1,), (1,)), ((), ())), preferred_element_type=F32)


def kernel(n, heads, hd,
           x_hbm, dy_hbm, gam_ref, bet_ref, wt_hbm, wo_hbm,
           y_hbm, dx_hbm, dwqkv_hbm, dwo_hbm, dg_ref, db_ref,
           xbuf, dybuf, wt, wo, w, xT, dyT, uT, qkvT, oT, mean_ref, rstd_ref, gb, bb,
           s_acc, comp, ar_in, ar_out, sx, sg, sgt, ubuf,
           acc, d2d, relay, fin, dgacc, dbacc, dgslots,
           sem_in, sem_out, ar_send, ar_recv, rs_send, rs_recv, dg_send, dg_recv):
    tokens, width = xbuf.shape
    steps = tokens // TT
    groups = 4
    hpg = heads // groups
    gr = hpg * hd
    nb = width // BLK
    chips = n // 2
    me = lax.axis_index("seq")
    chip, core = lax.div(me, 2), lax.rem(me, 2)
    partner = 2 * chip + (1 - core)
    c_right, c_left = lax.rem(chip + 1, chips), lax.rem(chip + chips - 1, chips)
    c_opp = lax.rem(chip + 2, chips)
    right, left = 2 * c_right + core, 2 * c_left + core

    def x_copy(t):
        r = pl.ds(pl.multiple_of(t * TT, TT), TT)
        return pltpu.make_async_copy(x_hbm.at[r, :], xbuf.at[r, :], sem_in.at[0, t])

    def dy_copy(t):
        r = pl.ds(pl.multiple_of(t * TT, TT), TT)
        return pltpu.make_async_copy(dy_hbm.at[r, :], dybuf.at[r, :], sem_in.at[1, t])

    wkv_copy = pltpu.make_async_copy(wt_hbm.at[pl.ds(width, 2 * width), :], wt.at[pl.ds(width, 2 * width), :], sem_in.at[2, 0])
    wq_copy = pltpu.make_async_copy(wt_hbm.at[pl.ds(0, width), :], wt.at[pl.ds(0, width), :], sem_in.at[2, 1])
    wo_copy = pltpu.make_async_copy(wo_hbm, wo, sem_in.at[2, 2])
    x_copy(0).start()
    wkv_copy.start()
    for t in range(1, steps):
        x_copy(t).start()
    for t in range(steps):
        dy_copy(t).start()
    wq_copy.start()
    wo_copy.start()

    barrier = pltpu.get_barrier_semaphore()
    for d in range(1, n):
        pl.semaphore_signal(barrier, inc=1, device_id={"seq": lax.rem(me + d, n)}, device_id_type=MESH)

    eye = (lax.broadcasted_iota(jnp.int32, (BLK, BLK), 0) == lax.broadcasted_iota(jnp.int32, (BLK, BLK), 1)).astype(F32).astype(BF16)
    gb[...] = jnp.transpose(jnp.broadcast_to(gam_ref[...][None, :], (128, width)))
    bb[...] = jnp.transpose(jnp.broadcast_to(bet_ref[...][None, :], (128, width)))
    s_acc[...] = jnp.zeros_like(s_acc)
    sx[...] = jnp.zeros_like(sx)
    dgacc[...] = jnp.zeros_like(dgacc)
    dbacc[...] = jnp.zeros_like(dbacc)

    def lanes(ref_val, tt=TT):
        return jnp.concatenate([ref_val] * (tt // 128), axis=1)

    def fold(v):
        out = v[:, :128]
        for i in range(1, TT // 128):
            out = out + v[:, 128 * i:128 * (i + 1)]
        return out

    def tok(t, tt=TT):
        return pl.ds(t * tt if isinstance(t, int) else pl.multiple_of(t * tt, tt), tt)

    def phi(v32):
        ex = jnp.exp(jnp.minimum(v32, 0.0))
        pos = v32 > 0
        return jnp.where(pos, v32 + 1.0, ex).astype(BF16), jnp.where(pos, 1.0, ex)

    def parts3(v):
        p1 = v.astype(BF16).astype(F32)
        r = v - p1
        p2 = r.astype(BF16).astype(F32)
        return p1, p2, (r - p2).astype(BF16).astype(F32)

    scope = jax.named_scope
    ones_rows = jnp.ones((BLK - gr, TT), BF16)

    def norm_tile(t):
        ts = tok(t)
        xt = jnp.concatenate([nt(eye, xbuf[ts, BLK * b:BLK * (b + 1)]) for b in range(nb)], axis=0)
        xT[:, ts] = xt.astype(BF16)
        mean = jnp.sum(xt, axis=0, keepdims=True) * (1.0 / width)
        cen = xt - mean
        var = jnp.sum(cen * cen, axis=0, keepdims=True) * (1.0 / width)
        rstd = lax.rsqrt(var + LN_EPS)
        mean_ref[:, ts] = mean
        rstd_ref[:, ts] = rstd
        u = (cen * rstd * lanes(gb[...]) + lanes(bb[...])).astype(BF16)
        uT[:, ts] = u
        ubuf[t % 2] = u

    def kv_mm(t, half, u):
        ts = tok(t)
        hw = width // 2
        kb = nn(wt[width + hw * half:width + hw * (half + 1), :], u[...]).astype(BF16)
        vb = nn(wt[2 * width + hw * half:2 * width + hw * (half + 1), :], u[...]).astype(BF16)
        qkvT[width + hw * half:width + hw * (half + 1), ts] = kb
        qkvT[2 * width + hw * half:2 * width + hw * (half + 1), ts] = vb
        return half, phi(kb.astype(F32))[0], vb

    def s_mm(half, fk, vb):
        for i, g in enumerate(half_groups(half)):
            rows = slice(gr * i, gr * (i + 1))
            s_acc[g] += nt(fk[rows], jnp.concatenate([vb[rows], ones_rows], axis=0))

    def half_groups(half):
        return range(groups // 2 * half, groups // 2 * (half + 1))

    lane128 = lax.broadcasted_iota(jnp.int32, (hd, 128), 1)
    lane256 = lax.broadcasted_iota(jnp.int32, (hd, BLK), 1)
    lane_sx = lax.broadcasted_iota(jnp.int32, (BLK, BLK), 1)
    rows_owned = hd // 2

    def compact(e, z_of):
        g0 = groups // 2 * (e % 2)

        def head(g, hh):
            blk = s_acc[g, hd * hh:hd * (hh + 1), :]
            moved = pltpu.roll(blk, BLK - hd * hh, axis=1) if hh else blk
            return jnp.where(lane128 < hd, moved[:, :128], jnp.where(lane128 == hd, z_of(hh, blk), 0.0))

        for j in range(hpg):
            pair = head(g0, j) + pltpu.roll(head(g0 + 1, j), 64, axis=1)
            comp[e, 2 * j] = pair[:rows_owned]
            comp[e, 2 * j + 1] = pair[rows_owned:]
        s_acc[g0:g0 + 2] = jnp.zeros((2, gr, BLK), F32)
        for d in range(1, n):
            ar1(e, d).start()

    def ar1(e, d):
        peer = lax.rem(me + d, n)
        return pltpu.make_async_remote_copy(
            src_ref=comp.at[e, peer], dst_ref=ar_in.at[e, d], send_sem=ar_send.at[2 * e, d], recv_sem=ar_recv.at[2 * e, d],
            device_id={"seq": peer}, device_id_type=MESH)

    def ar2(e, d):
        peer = lax.rem(me + d, n)
        return pltpu.make_async_remote_copy(
            src_ref=ar_out.at[e, 0], dst_ref=ar_out.at[e, d], send_sem=ar_send.at[2 * e + 1, d], recv_sem=ar_recv.at[2 * e + 1, d],
            device_id={"seq": peer}, device_id_type=MESH)

    def ar_reduce(i):
        total = comp[i, me]
        for d in range(1, n):
            ar1(i, d).wait_recv()
            total = total + ar_in[i, d]
        ar_out[i, 0] = total
        for d in range(1, n):
            ar2(i, d).start()

    def ar_finish(i):
        forward = i < 2
        for d in range(1, n):
            ar2(i, d).wait_recv()
        for g in half_groups(i % 2):
            for hh in range(hpg):
                part = jnp.concatenate([ar_out[i, lax.rem(me - p + n, n)] for p in (2 * hh, 2 * hh + 1)], axis=0)
                if g % 2:
                    part = pltpu.roll(part, 64, axis=1)
                wide = jnp.concatenate([jnp.where(lane128 < hd, part, 0.0), jnp.zeros((hd, 128), F32)], axis=1)
                if hh:
                    wide = pltpu.roll(wide, hd * hh, axis=1)
                zc = part[:, hd:hd + 1]
                if forward:
                    hit = (lane256 == gr + hh) | (lane256 == gr + hpg + hh) | (lane256 == gr + 2 * hpg + hh)
                    wide = jnp.where(hit, jnp.broadcast_to(zc, (hd, BLK)), wide)
                else:
                    for j, zp in enumerate(parts3(jnp.broadcast_to(zc, (hd, BLK)))):
                        wide = jnp.where(lane256 == gr + j, zp, wide)
                sx[hd * hh:hd * (hh + 1), :] = wide
            m = sx[...]
            ext = jnp.where(lane_sx >= gr, -m, m) if forward else m
            sg[g] = ext[:gr, :gr + 16].astype(BF16)
            sgt[g] = jnp.transpose(m)[:gr + 16, :gr].astype(BF16)

    def z_fwd(hh, blk):
        return blk[:, gr:gr + 1]

    off = lane128 - (gr - 128)

    def z_bwd(hh, blk):
        hit = (off >= 0) & (off < 3 * hpg) & (lax.rem(off, hpg) == hh)
        return -jnp.sum(jnp.where(hit, blk[:, 128:], 0.0), axis=1, keepdims=True)

    def do_half(half):
        @pl.loop(0, steps)
        def _(t):
            hw = width // 2
            acc[t, pl.ds(2 * half, 2), :, :, :TT] = nn(wo[hw * half:hw * (half + 1), :], dyT[:, tok(t)]).reshape(2, 2, gr // 2, TT)

    def q_tile(t):
        ts = tok(t)
        dy_copy(t).wait()
        for b in range(nb):
            dyT[BLK * b:BLK * (b + 1), ts] = nt(eye, dybuf[ts, BLK * b:BLK * (b + 1)]).astype(BF16)
        qkvT[0:width, ts] = nn(wt[0:width, :], uT[:, ts]).astype(BF16)

    with scope("A0"):
        x_copy(0).wait()
        norm_tile(0)
    wkv_copy.wait()
    for t in range(steps):
        with scope(f"A_{t}"):
            if t + 1 < steps:
                x_copy(t + 1).wait()
                norm_tile(t + 1)
            now = kv_mm(t, 0, ubuf.at[t % 2])
            if t:
                s_mm(*last)
            last = now
    with scope("A_s"):
        s_mm(*last)
    pl.semaphore_wait(barrier, n - 1)
    with scope("compact0"):
        compact(0, z_fwd)
    with scope("A2"):
        @pl.loop(0, steps)
        def _(t):
            s_mm(*kv_mm(t, 1, uT.at[:, tok(t)]))
    with scope("compact1"):
        compact(1, z_fwd)

    wq_copy.wait()
    with scope("fill_q0"):
        pl.loop(0, steps // 2)(q_tile)
    with scope("ar_reduce0"):
        ar_reduce(0)
    with scope("fill_q1"):
        pl.loop(steps // 2, steps)(q_tile)
    wo_copy.wait()
    with scope("do0"):
        do_half(0)
    with scope("ar_reduce1"):
        ar_reduce(1)
    with scope("ar_finish0"):
        ar_finish(0)

    def per_head(v):
        return jnp.broadcast_to(v[:, None, :], (hpg, hd, TT)).reshape(gr, TT)

    def b_tiles(i, half):
        pairs = [(i, g) for g in half_groups(half)]
        rows = {g: slice(gr * g, gr * (g + 1)) for _, g in pairs}
        feats = [phi(qkvT[rows[g], tok(t)].astype(F32)) for t, g in pairs]
        nds = [nn(sgt[g], fq) for (t, g), (fq, _) in zip(pairs, feats)]
        ges = []
        for (t, g), nd in zip(pairs, nds):
            rden = per_head(1.0 / nd[gr:gr + hpg])
            a = nd[:gr] * rden
            oT[rows[g], tok(t)] = a.astype(BF16)
            gg = (acc[t, g, :, :, :TT].reshape(gr, TT) * rden).astype(BF16)
            c = jnp.sum((gg.astype(F32) * a).reshape(hpg, hd, TT), axis=1)
            cp = jnp.concatenate(list(parts3(c)) + [jnp.zeros((hpg, TT), F32)], axis=0).astype(BF16)
            ges.append(jnp.concatenate([gg, cp], axis=0))
        dfqs = [nn(sg[g], ge) for (t, g), ge in zip(pairs, ges)]
        for (t, g), (fq, slope), ge, dfq in zip(pairs, feats, ges, dfqs):
            s_acc[g] += nt(fq, jnp.concatenate([ge, jnp.zeros((BLK - gr - 16, TT), BF16)], axis=0))
            qkvT[rows[g], tok(t)] = (dfq * slope).astype(BF16)

    own = width // n

    def grad(u):
        @pl.loop(0, 2)
        def _(m):
            half = lax.rem(lax.div(chip, 2) + 1 + m, 2)
            rs = pl.ds(pl.multiple_of(half * (width // 2), width // 2), width // 2)
            if u == 0:
                out = nn(oT[rs, :], dybuf[...])
            else:
                out = nt(uT[rs, :], qkvT[width * (u - 1):width * u, :])
            acc[u, pl.ds(2 * half, 2)] = out.reshape(2, 2, own, width)
            d2d_copy(u, 2 * half).start()
            d2d_copy(u, 2 * half + 1).start()

    hr = width // n // 2
    lo, hi = pl.ds(0, hr), pl.ds(hr, hr)

    def rdma(u, s, src, dst, peer):
        return pltpu.make_async_remote_copy(src_ref=src, dst_ref=dst, send_sem=rs_send.at[u, s], recv_sem=rs_recv.at[u, s],
                                            device_id={"seq": peer}, device_id_type=MESH)

    def d2d_copy(u, c):
        return rdma(u, c, acc.at[u, c, 1 - core], d2d.at[u, c], partner)

    def hop(u, s):
        if s == 0:
            return rdma(u, chips, acc.at[u, c_opp, core, lo], relay.at[u, 0], right)
        if s == 1:
            return rdma(u, chips + 1, acc.at[u, c_opp, core, hi], relay.at[u, 1], left)
        if s == 2:
            return rdma(u, chips + 2, acc.at[u, c_right, core, hi], fin.at[u, 0, hi], right)
        if s == 3:
            return rdma(u, chips + 3, acc.at[u, c_left, core, lo], fin.at[u, 1, lo], left)
        if s == 4:
            return rdma(u, chips + 4, acc.at[u, c_right, core, lo], fin.at[u, 0, lo], right)
        return rdma(u, chips + 5, acc.at[u, c_left, core, hi], fin.at[u, 1, hi], left)

    def rs_chip_a(u):
        d2d_copy(u, c_opp).wait_recv()
        acc[u, c_opp, core] += d2d[u, c_opp]
        hop(u, 0).start()
        hop(u, 1).start()

    def rs_chip_b(u):
        d2d_copy(u, c_right).wait_recv()
        acc[u, c_right, core] += d2d[u, c_right]
        hop(u, 2).start()
        d2d_copy(u, c_left).wait_recv()
        acc[u, c_left, core] += d2d[u, c_left]
        hop(u, 3).start()
        d2d_copy(u, chip).wait_recv()
        acc[u, chip, core] += d2d[u, chip]

    def rs_relay(u):
        hop(u, 0).wait_recv()
        acc[u, c_right, core, lo] += relay[u, 0]
        hop(u, 4).start()
        hop(u, 1).wait_recv()
        acc[u, c_left, core, hi] += relay[u, 1]
        hop(u, 5).start()

    def out_copy(u):
        dst = dwo_hbm if u == 0 else dwqkv_hbm.at[:, pl.ds(width * (u - 1), width)]
        return pltpu.make_async_copy(acc.at[u, chip, core], dst, sem_out.at[2, u])

    def rs_final(u):
        for s in range(2, 6):
            hop(u, s).wait_recv()
        acc[u, chip, core] += fin[u, 0] + fin[u, 1]
        out_copy(u).start()

    def y_copy(t):
        r = tok(t)
        return pltpu.make_async_copy(xbuf.at[r, :], y_hbm.at[r, :], sem_out.at[0, t])

    def dx_copy(t):
        r = tok(t)
        return pltpu.make_async_copy(dybuf.at[r, :], dx_hbm.at[r, :], sem_out.at[1, t])

    def store_tokens(buf, t, val):
        for s in range(TT // BLK):
            r = pl.ds(t * TT + BLK * s if isinstance(t, int) else pl.multiple_of(t * TT + BLK * s, BLK), BLK)
            for b in range(nb):
                buf[r, BLK * b:BLK * (b + 1)] = nt(eye, val[BLK * b:BLK * (b + 1), BLK * s:BLK * (s + 1)]).astype(BF16)

    def y_tile(t):
        ts = tok(t)
        yt = (nn(uT[:, 0:width], oT[:, ts]) + xT[:, ts].astype(F32)).astype(BF16)
        store_tokens(xbuf, t, yt)
        y_copy(t).start()

    def c_tiles(i, half):
        pairs = [(2 * i + k, g) for k in range(2) for g in half_groups(half)]
        krows = {g: slice(width + gr * g, width + gr * (g + 1)) for _, g in pairs}
        vrows = {g: slice(2 * width + gr * g, 2 * width + gr * (g + 1)) for _, g in pairs}
        dfks = [nn(sg[g], jnp.concatenate([qkvT[vrows[g], tok(t)], ones_rows[:16]], axis=0)) for t, g in pairs]
        feats = [phi(qkvT[krows[g], tok(t)].astype(F32)) for t, g in pairs]
        dvs = [nn(sgt[g, :gr, :], fk) for (t, g), (fk, _) in zip(pairs, feats)]
        for (t, g), (_, slope), dfk, dv in zip(pairs, feats, dfks, dvs):
            qkvT[krows[g], tok(t)] = (dfk * slope).astype(BF16)
            qkvT[vrows[g], tok(t)] = dv.astype(BF16)

    def du_tile(t):
        i = 2 * (t % 2)
        d2d[i:i + 2, :, :, :TT] = nn(w[...], qkvT[:, tok(t)]).reshape(2, chips, own, TT)

    def dx_tile(t):
        ts = tok(t)
        i = 2 * (t % 2)
        du = d2d[i:i + 2, :, :, :TT].reshape(width, TT)
        rstd = rstd_ref[:, ts]
        xhat = (xT[:, ts].astype(F32) - mean_ref[:, ts]) * rstd
        p = du * xhat
        dgacc[...] += fold(p)
        dbacc[...] += fold(du)
        gl = lanes(gb[...])
        e = du * gl
        m1 = jnp.sum(e, axis=0, keepdims=True) * (1.0 / width)
        m2 = jnp.sum(p * gl, axis=0, keepdims=True) * (1.0 / width)
        dxt = (dyT[:, ts].astype(F32) + rstd * (e - m1 - xhat * m2)).astype(BF16)
        store_tokens(dybuf, t, dxt)

    with scope("B0"):
        pl.loop(0, steps)(functools.partial(b_tiles, half=0))
    with scope("compact2"):
        compact(2, z_bwd)
    with scope("do1"):
        do_half(1)
    with scope("ar_finish1"):
        ar_finish(1)
    with scope("B1"):
        pl.loop(0, steps)(functools.partial(b_tiles, half=1))
    with scope("compact3"):
        compact(3, z_bwd)
    with scope("ar_reduce2"):
        ar_reduce(2)
    with scope("gradwo"):
        grad(0)
    with scope("rs_chip_a0"):
        rs_chip_a(0)
    with scope("ar_reduce3"):
        ar_reduce(3)
    with scope("rs_chip_b0"):
        rs_chip_b(0)
    with scope("gradwq"):
        grad(1)
    with scope("ar_finish2"):
        ar_finish(2)
    with scope("C0"):
        pl.loop(0, steps // 2)(functools.partial(c_tiles, half=0))
    with scope("ar_finish3"):
        ar_finish(3)
    with scope("relay0"):
        rs_relay(0)
        rs_chip_a(1)
    with scope("C1"):
        pl.loop(0, steps // 2)(functools.partial(c_tiles, half=1))
    with scope("rs_chip_b1"):
        rs_chip_b(1)
    with scope("gradwk"):
        grad(2)
    with scope("rs_chip_a2"):
        rs_chip_a(2)
        rs_chip_b(2)
    with scope("gradwv"):
        grad(3)
    with scope("relay1"):
        rs_relay(1)
    wot = uT.at[:, 0:width]
    with scope("fill_wo"):
        for i in range(nb):
            for j in range(nb):
                wot[BLK * j:BLK * (j + 1), BLK * i:BLK * (i + 1)] = nt(eye, wo[BLK * i:BLK * (i + 1), BLK * j:BLK * (j + 1)]).astype(BF16)
    with scope("fill_w"):
        @pl.loop(0, 3 * nb)
        def _(j):
            js = pl.ds(pl.multiple_of(j * BLK, BLK), BLK)
            for i in range(nb):
                w[BLK * i:BLK * (i + 1), js] = nt(eye, wt[js, BLK * i:BLK * (i + 1)]).astype(BF16)
    with scope("rs_chip3"):
        rs_chip_a(3)
        rs_chip_b(3)
    for t in range(steps + 1):
        with scope(f"DU_{t}"):
            if t < steps:
                du_tile(t)
            if t > 0:
                dx_tile(t - 1)
                dx_copy(t - 1).start()
        if t == 2:
            with scope("relay2"):
                rs_relay(2)

    def dg_copy(d):
        return pltpu.make_async_remote_copy(
            src_ref=dgslots.at[0], dst_ref=dgslots.at[d], send_sem=dg_send.at[d], recv_sem=dg_recv.at[d],
            device_id={"seq": lax.rem(me + d, n)}, device_id_type=MESH)

    dgrow = jnp.sum(jnp.transpose(dgacc[...]), axis=0, keepdims=True)
    dbrow = jnp.sum(jnp.transpose(dbacc[...]), axis=0, keepdims=True)
    dgslots[0] = jnp.concatenate([dgrow, dbrow], axis=0)
    for d in range(1, n):
        dg_copy(d).start()

    with scope("relay3"):
        rs_relay(3)
    with scope("final"):
        for u in range(3):
            rs_final(u)
    with scope("Y"):
        pl.loop(0, steps)(y_tile)
    with scope("final3"):
        rs_final(3)

    for d in range(1, n):
        dg_copy(d).wait_recv()
    total = dgslots[lax.rem(me, n)]
    for p in range(1, n):
        total = total + dgslots[lax.rem(me - p + n, n)]
    dg_ref[...] = total[0]
    db_ref[...] = total[1]

    for d in range(1, n):
        for e in range(4):
            ar1(e, d).wait_send()
            ar2(e, d).wait_send()
        dg_copy(d).wait_send()
    for u in range(4):
        out_copy(u).wait()
        for c in range(chips):
            d2d_copy(u, c).wait_send()
        for s in range(6):
            hop(u, s).wait_send()

    @pl.loop(0, steps)
    def _(t):
        y_copy(t).wait()
        dx_copy(t).wait()


def local_block(n, x_tok, dy_tok, ln_gamma, ln_beta, w_qkv, w_out):
    tokens, width = x_tok.shape
    _, three, heads, hd = w_qkv.shape
    wt = w_qkv.transpose(1, 2, 3, 0).reshape(three * width, width)
    steps = tokens // TT
    chips = n // 2
    own = width // n
    hbm = pl.BlockSpec(memory_space=pl.ANY)
    vmem = pl.BlockSpec(memory_space=pltpu.VMEM)
    gr = heads * hd // 4
    dma = pltpu.SemaphoreType.DMA
    y, dx, dwqkv, dwo, dg, db = pl.pallas_call(
        functools.partial(kernel, n, heads, hd),
        name="block",
        out_shape=(
            jax.ShapeDtypeStruct((tokens, width), BF16), jax.ShapeDtypeStruct((tokens, width), BF16),
            jax.ShapeDtypeStruct((own, three * width), F32), jax.ShapeDtypeStruct((own, width), F32),
            jax.ShapeDtypeStruct((width,), F32), jax.ShapeDtypeStruct((width,), F32)),
        in_specs=[hbm, hbm, vmem, vmem, hbm, hbm],
        out_specs=(hbm, hbm, hbm, hbm, vmem, vmem),
        scratch_shapes=[
            pltpu.VMEM((tokens, width), BF16), pltpu.VMEM((tokens, width), BF16),
            pltpu.VMEM((three * width, width), BF16), pltpu.VMEM((width, width), BF16),
            pltpu.VMEM((width, three * width), BF16),
            pltpu.VMEM((width, tokens), BF16), pltpu.VMEM((width, tokens), BF16), pltpu.VMEM((width, tokens), BF16),
            pltpu.VMEM((three * width, tokens), BF16), pltpu.VMEM((width, tokens), BF16),
            pltpu.VMEM((1, tokens), F32), pltpu.VMEM((1, tokens), F32),
            pltpu.VMEM((width, 128), F32), pltpu.VMEM((width, 128), F32),
            pltpu.VMEM((4, gr, BLK), F32), pltpu.VMEM((4, n, hd // 2, 128), F32),
            pltpu.VMEM((4, n, hd // 2, 128), F32), pltpu.VMEM((4, n, hd // 2, 128), F32),
            pltpu.VMEM((BLK, BLK), F32), pltpu.VMEM((4, gr, gr + 16), BF16), pltpu.VMEM((4, gr + 16, gr), BF16),
            pltpu.VMEM((2, width, TT), BF16),
            pltpu.VMEM((4, chips, 2, own, width), F32), pltpu.VMEM((4, chips, own, width), F32),
            pltpu.VMEM((4, 2, own // 2, width), F32), pltpu.VMEM((4, 2, own, width), F32),
            pltpu.VMEM((width, 128), F32), pltpu.VMEM((width, 128), F32), pltpu.VMEM((n, 2, width), F32),
            dma((3, max(steps, 3))), dma((3, max(steps, 4))),
            dma((8, n)), dma((8, n)), dma((4, chips + 6)), dma((4, chips + 6)), dma((n,)), dma((n,)),
        ],
        compiler_params=pltpu.CompilerParams(collective_id=0, has_side_effects=True, vmem_limit_bytes=67_000_000),
    )(x_tok, dy_tok, ln_gamma, ln_beta, wt, w_out)
    return y, dx, dwqkv.reshape(own, three, heads, hd), dwo, dg, db


def solution(mesh):
    rows = P(("data", "seq"), None)
    return jax.shard_map(
        functools.partial(local_block, mesh.shape["seq"]), mesh=mesh,
        in_specs=(rows, rows, P(None), P(None), P(None, None, None, None), P(None, None)),
        out_specs=(rows, rows, P(("data", "seq"), None, None, None), rows, P("data"), P("data")),
        check_vma=False)
```

time: 107 us -> 94.8 us (0.89)
  Pallas kernels: 92.1 us -> 84 us
  other arithmetic: 2.55 us -> 0 us
  local copies, waits for them, and re-layouts: 11.4 us -> 10 us
    pallas_call x1, Pallas kernels: 92.1 us -> 84 us  [local_block(): pl.pallas_call(functools.partial(kernel, n, heads, hd), name='block', out...]
    pallas_call x2 -> x0, other arithmetic: 2.55 us -> none  [local_block(): pl.pallas_call(functools.partial(kernel, n, heads, hd), name='block', out...]
    reshape x2 -> x0, local copies, waits for them, and re-layouts: 2.53 us -> none  [the longest x1 1.27 us: local_block(): ln_gamma.reshape(1, width)]
    unnamed x7 -> x13, local copies, waits for them, and re-layouts: 6.29 us -> 7.49 us
where the time goes in v1:
time: 94.8 us; the launch traced here: 94.7 us
  Pallas kernels  84 us (89%)
  local copies, waits for them, and re-layouts  10 us (11%)
    pallas_call x1, Pallas kernels, local_block(): pl.pallas_call(functools.partial(kernel, n, heads, hd), name='block', out...  84 us
    unnamed x13, local copies, waits for them, and re-layouts  7.49 us
    pallas_call x1, local copies, waits for them, and re-layouts, local_block(): pl.pallas_call(functools.partial(kernel, n, heads, hd), name='block', out...  2.55 us

profile of v1, /device:TPU:113, one launch (start us, length us, event | category | flops | bytes accessed | tf_op | source)
XLA Modules:
  0.0 94.7 jit_solution(8059900837995678971)
XLA Ops:
  0.6 84.0 %block.1 = (bf16[2048,768]{1,0:T(8,128)(2,1)}, bf16[2048,768]{1,0:T(8,128)(2,1)}, f32[96,2304]{1,0:T(8,128)}, f32[96,768]{1,0:T(8,128)}, f32[768]{0:T(1024)}, /*index=5*/f32[768]{0:T(1024)}) custom-call(bf16[2048,768]{1,0:T(8,128)(2,1)} %x_hbm.1, bf16[2048,768]{1,0:T(8,128)(2,1)} %dy_hbm.1, f32[768]{0:T(1024)} %gam_ref.1, f32[768]{0:T(1024)} %bet_ref.1, ...), custom_call_target="tpu_custom_call" | custom-call | tf_op jit(solution)/shard_map/block/pallas_call | solution.py:539
  84.6 2.6 %copy.13 = f32[96,2304]{0,1:T(8,128)} copy(f32[96,2304]{1,0:T(8,128)} %get-tuple-element.14) | data formatting | bytes 1769472 | tf_op jit(solution)/shard_map/block/pallas_call | solution.py:539
  87.2 0.0 copy-start
  87.2 3.9 %copy.19 = bf16[2048,768]{1,0:T(8,128)(2,1)} copy(bf16[2048,768]{1,0:T(8,128)(2,1)} %get-tuple-element.30) | data formatting | bytes 6291456
  91.1 0.0 copy-done
  91.1 0.0 copy-start.1
  91.1 0.0 copy-start.3
  91.1 0.0 copy-start.2
  91.1 1.7 %copy.20 = bf16[2048,768]{1,0:T(8,128)(2,1)} copy(bf16[2048,768]{1,0:T(8,128)(2,1)S(1)} %copy-done) | data formatting | bytes 6291456
  92.8 0.0 copy-done.1
  92.8 0.7 copy.21
  93.5 0.0 copy-done.3
  93.5 0.6 copy.22
  94.1 0.0 copy-done.2
  94.1 0.6 copy.23
Async XLA Ops:
  87.2 3.9 %copy-start = (bf16[2048,768]{1,0:T(8,128)(2,1)S(1)}, bf16[2048,768]{1,0:T(8,128)(2,1)}, u32[]{:S(2)}) copy-start(bf16[2048,768]{1,0:T(8,128)(2,1)} %get-tuple-element.31) | copy-start | bytes 9437188
  91.1 1.7 %copy-start.1 = (f32[96,768]{1,0:T(8,128)S(1)}, f32[96,768]{1,0:T(8,128)}, u32[]{:S(2)}) copy-start(f32[96,768]{1,0:T(8,128)} %get-tuple-element.33) | copy-start | bytes 884740
  91.1 2.4 %copy-start.3 = (f32[768]{0:T(1024)S(1)}, f32[768]{0:T(1024)}, u32[]{:S(2)}) copy-start(f32[768]{0:T(1024)} %get-tuple-element.34) | copy-start | bytes 9220
  91.1 3.0 %copy-start.2 = (f32[768]{0:T(1024)S(1)}, f32[768]{0:T(1024)}, u32[]{:S(2)}) copy-start(f32[768]{0:T(1024)} %get-tuple-element.35) | copy-start | bytes 9220

commit v2 on v1

--- a/solution.py
+++ b/solution.py
@@ -25,10 +25,10 @@
 
 def kernel(n, heads, hd,
            x_hbm, dy_hbm, gam_ref, bet_ref, wt_hbm, wo_hbm,
-           y_hbm, dx_hbm, dwqkv_hbm, dwo_hbm, dg_ref, db_ref,
-           xbuf, dybuf, wt, wo, w, xT, dyT, uT, qkvT, oT, mean_ref, rstd_ref, gb, bb,
+           y_hbm, dx_hbm, dwqkv_hbm, dwo_hbm, dg_hbm, db_hbm,
+           xbuf, dybuf, wt, wo, xT, dyT, uT, qkvT, oT, mean_ref, rstd_ref, gb, bb,
            s_acc, comp, ar_in, ar_out, sx, sg, sgt, ubuf,
-           acc, d2d, relay, fin, dgacc, dbacc, dgslots,
+           acc, d2d, relay, fin, dgacc, dgslots, dgout, dbout,
            sem_in, sem_out, ar_send, ar_recv, rs_send, rs_recv, dg_send, dg_recv):
     tokens, width = xbuf.shape
     steps = tokens // TT
@@ -74,7 +74,6 @@
     s_acc[...] = jnp.zeros_like(s_acc)
     sx[...] = jnp.zeros_like(sx)
     dgacc[...] = jnp.zeros_like(dgacc)
-    dbacc[...] = jnp.zeros_like(dbacc)
 
     def lanes(ref_val, tt=TT):
         return jnp.concatenate([ref_val] * (tt // 128), axis=1)
@@ -128,7 +127,7 @@
     def s_mm(half, fk, vb):
         for i, g in enumerate(half_groups(half)):
             rows = slice(gr * i, gr * (i + 1))
-            s_acc[g] += nt(fk[rows], jnp.concatenate([vb[rows], ones_rows], axis=0))
+            s_acc[g % 2] += nt(fk[rows], jnp.concatenate([vb[rows], ones_rows], axis=0))
 
     def half_groups(half):
         return range(groups // 2 * half, groups // 2 * (half + 1))
@@ -142,38 +141,43 @@
         g0 = groups // 2 * (e % 2)
 
         def head(g, hh):
-            blk = s_acc[g, hd * hh:hd * (hh + 1), :]
+            blk = s_acc[g % 2, hd * hh:hd * (hh + 1), :]
             moved = pltpu.roll(blk, BLK - hd * hh, axis=1) if hh else blk
             return jnp.where(lane128 < hd, moved[:, :128], jnp.where(lane128 == hd, z_of(hh, blk), 0.0))
 
+        if e >= 2:
+            for d in range(1, n):
+                ar1(e - 2, d).wait_send()
         for j in range(hpg):
             pair = head(g0, j) + pltpu.roll(head(g0 + 1, j), 64, axis=1)
-            comp[e, 2 * j] = pair[:rows_owned]
-            comp[e, 2 * j + 1] = pair[rows_owned:]
-        s_acc[g0:g0 + 2] = jnp.zeros((2, gr, BLK), F32)
+            comp[e % 2, 2 * j] = pair[:rows_owned]
+            comp[e % 2, 2 * j + 1] = pair[rows_owned:]
+        s_acc[...] = jnp.zeros_like(s_acc)
         for d in range(1, n):
             ar1(e, d).start()
 
     def ar1(e, d):
         peer = lax.rem(me + d, n)
         return pltpu.make_async_remote_copy(
-            src_ref=comp.at[e, peer], dst_ref=ar_in.at[e, d], send_sem=ar_send.at[2 * e, d], recv_sem=ar_recv.at[2 * e, d],
+            src_ref=comp.at[e % 2, peer], dst_ref=ar_in.at[e % 2, d], send_sem=ar_send.at[2 * e, d], recv_sem=ar_recv.at[2 * e, d],
             device_id={"seq": peer}, device_id_type=MESH)
 
     def ar2(e, d):
         peer = lax.rem(me + d, n)
         return pltpu.make_async_remote_copy(
-            src_ref=ar_out.at[e, 0], dst_ref=ar_out.at[e, d], send_sem=ar_send.at[2 * e + 1, d], recv_sem=ar_recv.at[2 * e + 1, d],
+            src_ref=ar_out.at[e % 2, 0], dst_ref=ar_out.at[e % 2, d], send_sem=ar_send.at[2 * e + 1, d], recv_sem=ar_recv.at[2 * e + 1, d],
             device_id={"seq": peer}, device_id_type=MESH)
 
-    def ar_reduce(i):
-        total = comp[i, me]
+    def ar_reduce(e):
+        total = comp[e % 2, me]
         for d in range(1, n):
-            ar1(i, d).wait_recv()
-            total = total + ar_in[i, d]
-        ar_out[i, 0] = total
+            ar1(e, d).wait_recv()
+            total = total + ar_in[e % 2, d]
+            if e >= 2:
+                ar2(e - 2, d).wait_send()
+        ar_out[e % 2, 0] = total
         for d in range(1, n):
-            ar2(i, d).start()
+            ar2(e, d).start()
 
     def ar_finish(i):
         forward = i < 2
@@ -181,7 +185,7 @@
             ar2(i, d).wait_recv()
         for g in half_groups(i % 2):
             for hh in range(hpg):
-                part = jnp.concatenate([ar_out[i, lax.rem(me - p + n, n)] for p in (2 * hh, 2 * hh + 1)], axis=0)
+                part = jnp.concatenate([ar_out[i % 2, lax.rem(me - p + n, n)] for p in (2 * hh, 2 * hh + 1)], axis=0)
                 if g % 2:
                     part = pltpu.roll(part, 64, axis=1)
                 wide = jnp.concatenate([jnp.where(lane128 < hd, part, 0.0), jnp.zeros((hd, 128), F32)], axis=1)
@@ -209,11 +213,8 @@
         hit = (off >= 0) & (off < 3 * hpg) & (lax.rem(off, hpg) == hh)
         return -jnp.sum(jnp.where(hit, blk[:, 128:], 0.0), axis=1, keepdims=True)
 
-    def do_half(half):
-        @pl.loop(0, steps)
-        def _(t):
-            hw = width // 2
-            acc[t, pl.ds(2 * half, 2), :, :, :TT] = nn(wo[hw * half:hw * (half + 1), :], dyT[:, tok(t)]).reshape(2, 2, gr // 2, TT)
+    def do_tile(t):
+        acc[t, pl.ds(0, 2), :, :, :TT] = nn(wo[:width // 2, :], dyT[:, tok(t)]).reshape(2, 2, gr // 2, TT)
 
     def q_tile(t):
         ts = tok(t)
@@ -249,14 +250,14 @@
 
     wq_copy.wait()
     with scope("fill_q0"):
-        pl.loop(0, steps // 2)(q_tile)
+        q_tile(0)
     with scope("ar_reduce0"):
         ar_reduce(0)
     with scope("fill_q1"):
-        pl.loop(steps // 2, steps)(q_tile)
+        pl.loop(1, steps)(q_tile)
     wo_copy.wait()
     with scope("do0"):
-        do_half(0)
+        pl.loop(0, steps)(do_tile)
     with scope("ar_reduce1"):
         ar_reduce(1)
     with scope("ar_finish0"):
@@ -264,31 +265,40 @@
 
     def per_head(v):
         return jnp.broadcast_to(v[:, None, :], (hpg, hd, TT)).reshape(gr, TT)
+
+    def o_tiles(i, half):
+        nds = [nn(sgt[g], phi(qkvT[gr * g:gr * (g + 1), tok(i)].astype(F32))[0]) for g in half_groups(half)]
+        for g, nd in zip(half_groups(half), nds):
+            oT[gr * g:gr * (g + 1), tok(i)] = (nd[:gr] * per_head(1.0 / nd[gr:gr + hpg])).astype(BF16)
 
     def b_tiles(i, half):
         pairs = [(i, g) for g in half_groups(half)]
         rows = {g: slice(gr * g, gr * (g + 1)) for _, g in pairs}
         feats = [phi(qkvT[rows[g], tok(t)].astype(F32)) for t, g in pairs]
         nds = [nn(sgt[g], fq) for (t, g), (fq, _) in zip(pairs, feats)]
+        dos = [acc[t, g, :, :, :TT].reshape(gr, TT) if half == 0 else nn(wo[rows[g], :], dyT[:, tok(t)]) for t, g in pairs]
         ges = []
-        for (t, g), nd in zip(pairs, nds):
+        for (t, g), nd, do in zip(pairs, nds, dos):
             rden = per_head(1.0 / nd[gr:gr + hpg])
             a = nd[:gr] * rden
-            oT[rows[g], tok(t)] = a.astype(BF16)
-            gg = (acc[t, g, :, :, :TT].reshape(gr, TT) * rden).astype(BF16)
+            if half == 0:
+                oT[rows[g], tok(t)] = a.astype(BF16)
+            gg = (do * rden).astype(BF16)
             c = jnp.sum((gg.astype(F32) * a).reshape(hpg, hd, TT), axis=1)
             cp = jnp.concatenate(list(parts3(c)) + [jnp.zeros((hpg, TT), F32)], axis=0).astype(BF16)
             ges.append(jnp.concatenate([gg, cp], axis=0))
         dfqs = [nn(sg[g], ge) for (t, g), ge in zip(pairs, ges)]
         for (t, g), (fq, slope), ge, dfq in zip(pairs, feats, ges, dfqs):
-            s_acc[g] += nt(fq, jnp.concatenate([ge, jnp.zeros((BLK - gr - 16, TT), BF16)], axis=0))
+            s_acc[g % 2] += nt(fq, jnp.concatenate([ge, jnp.zeros((BLK - gr - 16, TT), BF16)], axis=0))
             qkvT[rows[g], tok(t)] = (dfq * slope).astype(BF16)
 
     own = width // n
 
-    def grad(u):
+    def grad(u, between=None):
         @pl.loop(0, 2)
         def _(m):
+            if between is not None:
+                pl.when(m == 1)(between)
             half = lax.rem(lax.div(chip, 2) + 1 + m, 2)
             rs = pl.ds(pl.multiple_of(half * (width // 2), width // 2), width // 2)
             if u == 0:
@@ -347,13 +357,18 @@
         hop(u, 5).start()
 
     def out_copy(u):
-        dst = dwo_hbm if u == 0 else dwqkv_hbm.at[:, pl.ds(width * (u - 1), width)]
-        return pltpu.make_async_copy(acc.at[u, chip, core], dst, sem_out.at[2, u])
+        if u == 0:
+            return pltpu.make_async_copy(acc.at[u, chip, core], dwo_hbm, sem_out.at[2, u])
+        return pltpu.make_async_copy((gb, dgacc, bb)[u - 1], dwqkv_hbm.at[pl.ds(width * (u - 1), width), :], sem_out.at[2, u])
 
     def rs_final(u):
         for s in range(2, 6):
             hop(u, s).wait_recv()
-        acc[u, chip, core] += fin[u, 0] + fin[u, 1]
+        total = acc[u, chip, core] + fin[u, 0] + fin[u, 1]
+        if u == 0:
+            acc[u, chip, core] = total
+        else:
+            (gb, dgacc, bb)[u - 1][:, :own] = jnp.transpose(total)
         out_copy(u).start()
 
     def y_copy(t):
@@ -372,7 +387,7 @@
 
     def y_tile(t):
         ts = tok(t)
-        yt = (nn(uT[:, 0:width], oT[:, ts]) + xT[:, ts].astype(F32)).astype(BF16)
+        yt = (nn(ubuf[0], oT[:TT, ts]) + nn(ubuf[1, :, :width - TT], oT[TT:, ts]) + xT[:, ts].astype(F32)).astype(BF16)
         store_tokens(xbuf, t, yt)
         y_copy(t).start()
 
@@ -389,7 +404,7 @@
 
     def du_tile(t):
         i = 2 * (t % 2)
-        d2d[i:i + 2, :, :, :TT] = nn(w[...], qkvT[:, tok(t)]).reshape(2, chips, own, TT)
+        d2d[i:i + 2, :, :, :TT] = (nn(dyT[...], qkvT[:tokens, tok(t)]) + nn(ubuf[1, :, BLK:], qkvT[tokens:, tok(t)])).reshape(2, chips, own, TT)
 
     def dx_tile(t):
         ts = tok(t)
@@ -399,74 +414,87 @@
         xhat = (xT[:, ts].astype(F32) - mean_ref[:, ts]) * rstd
         p = du * xhat
         dgacc[...] += fold(p)
-        dbacc[...] += fold(du)
+        bb[...] += fold(du)
         gl = lanes(gb[...])
         e = du * gl
         m1 = jnp.sum(e, axis=0, keepdims=True) * (1.0 / width)
         m2 = jnp.sum(p * gl, axis=0, keepdims=True) * (1.0 / width)
-        dxt = (dyT[:, ts].astype(F32) + rstd * (e - m1 - xhat * m2)).astype(BF16)
+        dyt = jnp.concatenate([nt(eye, dybuf[ts, BLK * b:BLK * (b + 1)]) for b in range(nb)], axis=0)
+        dxt = (dyt + rstd * (e - m1 - xhat * m2)).astype(BF16)
         store_tokens(dybuf, t, dxt)
+
+    def w_block(j):
+        js = pl.ds(pl.multiple_of(j * BLK, BLK), BLK)
+        for i in range(nb):
+            dyT[BLK * i:BLK * (i + 1), js] = nt(eye, wt[js, BLK * i:BLK * (i + 1)]).astype(BF16)
+
+    def w_rest():
+        for i in range(nb):
+            ubuf[1, BLK * i:BLK * (i + 1), BLK:] = nt(eye, wt[tokens:, BLK * i:BLK * (i + 1)]).astype(BF16)
 
     with scope("B0"):
         pl.loop(0, steps)(functools.partial(b_tiles, half=0))
     with scope("compact2"):
         compact(2, z_bwd)
-    with scope("do1"):
-        do_half(1)
     with scope("ar_finish1"):
         ar_finish(1)
+    with scope("O1"):
+        pl.loop(0, steps)(functools.partial(o_tiles, half=1))
+    with scope("gradwo"):
+        grad(0)
+    with scope("ar_reduce2"):
+        ar_reduce(2)
+    with scope("rs_chip_a0"):
+        rs_chip_a(0)
     with scope("B1"):
-        pl.loop(0, steps)(functools.partial(b_tiles, half=1))
+        @pl.loop(0, steps)
+        def _(t):
+            @pl.when(t == steps // 2)
+            def _():
+                rs_chip_b(0)
+            b_tiles(t, half=1)
     with scope("compact3"):
         compact(3, z_bwd)
-    with scope("ar_reduce2"):
-        ar_reduce(2)
-    with scope("gradwo"):
-        grad(0)
-    with scope("rs_chip_a0"):
-        rs_chip_a(0)
+    with scope("fill_w"):
+        pl.loop(0, tokens // BLK)(w_block)
+        w_rest()
+    with scope("relay0"):
+        rs_relay(0)
+    with scope("gradwq"):
+        grad(1)
     with scope("ar_reduce3"):
         ar_reduce(3)
-    with scope("rs_chip_b0"):
-        rs_chip_b(0)
-    with scope("gradwq"):
-        grad(1)
+    with scope("chip_a1"):
+        rs_chip_a(1)
     with scope("ar_finish2"):
         ar_finish(2)
     with scope("C0"):
         pl.loop(0, steps // 2)(functools.partial(c_tiles, half=0))
+    with scope("rs_chip_b1"):
+        rs_chip_b(1)
+    with scope("fill_wo"):
+        for i in range(nb):
+            for j in range(nb):
+                k = BLK * i // TT
+                ubuf[k, BLK * j:BLK * (j + 1), BLK * i - TT * k:BLK * (i + 1) - TT * k] = nt(
+                    eye, wo[BLK * i:BLK * (i + 1), BLK * j:BLK * (j + 1)]).astype(BF16)
+    with scope("Y0"):
+        pl.loop(0, steps // 2)(y_tile)
     with scope("ar_finish3"):
         ar_finish(3)
-    with scope("relay0"):
-        rs_relay(0)
-        rs_chip_a(1)
     with scope("C1"):
         pl.loop(0, steps // 2)(functools.partial(c_tiles, half=1))
-    with scope("rs_chip_b1"):
-        rs_chip_b(1)
+    with scope("relay1"):
+        rs_relay(1)
     with scope("gradwk"):
         grad(2)
     with scope("rs_chip_a2"):
         rs_chip_a(2)
-        rs_chip_b(2)
     with scope("gradwv"):
-        grad(3)
-    with scope("relay1"):
-        rs_relay(1)
-    wot = uT.at[:, 0:width]
-    with scope("fill_wo"):
-        for i in range(nb):
-            for j in range(nb):
-                wot[BLK * j:BLK * (j + 1), BLK * i:BLK * (i + 1)] = nt(eye, wo[BLK * i:BLK * (i + 1), BLK * j:BLK * (j + 1)]).astype(BF16)
-    with scope("fill_w"):
-        @pl.loop(0, 3 * nb)
-        def _(j):
-            js = pl.ds(pl.multiple_of(j * BLK, BLK), BLK)
-            for i in range(nb):
-                w[BLK * i:BLK * (i + 1), js] = nt(eye, wt[js, BLK * i:BLK * (i + 1)]).astype(BF16)
-    with scope("rs_chip3"):
+        grad(3, lambda: rs_chip_b(2))
+    with scope("rs_chip_a3"):
         rs_chip_a(3)
-        rs_chip_b(3)
+    bb[...] = jnp.zeros_like(bb)
     for t in range(steps + 1):
         with scope(f"DU_{t}"):
             if t < steps:
@@ -474,9 +502,13 @@
             if t > 0:
                 dx_tile(t - 1)
                 dx_copy(t - 1).start()
+        if t == 0:
+            with scope("relay2"):
+                rs_chip_b(3)
+                rs_relay(2)
         if t == 2:
-            with scope("relay2"):
-                rs_relay(2)
+            with scope("relay3"):
+                rs_relay(3)
 
     def dg_copy(d):
         return pltpu.make_async_remote_copy(
@@ -484,31 +516,38 @@
             device_id={"seq": lax.rem(me + d, n)}, device_id_type=MESH)
 
     dgrow = jnp.sum(jnp.transpose(dgacc[...]), axis=0, keepdims=True)
-    dbrow = jnp.sum(jnp.transpose(dbacc[...]), axis=0, keepdims=True)
+    dbrow = jnp.sum(jnp.transpose(bb[...]), axis=0, keepdims=True)
     dgslots[0] = jnp.concatenate([dgrow, dbrow], axis=0)
     for d in range(1, n):
         dg_copy(d).start()
 
-    with scope("relay3"):
-        rs_relay(3)
+    def dg_out(i):
+        return pltpu.make_async_copy((dgout, dbout)[i], (dg_hbm, db_hbm)[i], sem_out.at[3, i])
+
     with scope("final"):
-        for u in range(3):
-            rs_final(u)
-    with scope("Y"):
-        pl.loop(0, steps)(y_tile)
+        rs_final(0)
+        rs_final(1)
+    with scope("Y1"):
+        pl.loop(steps // 2, steps)(y_tile)
+    with scope("final2"):
+        rs_final(2)
     with scope("final3"):
         rs_final(3)
 
+    with scope("dg"):
+        for d in range(1, n):
+            dg_copy(d).wait_recv()
+        total = dgslots[me]
+        for p in range(1, n):
+            total = total + dgslots[lax.rem(me - p + n, n)]
+        dgout[...] = total[0]
+        dbout[...] = total[1]
+        dg_out(0).start()
+        dg_out(1).start()
+    dg_out(0).wait()
+    dg_out(1).wait()
     for d in range(1, n):
-        dg_copy(d).wait_recv()
-    total = dgslots[lax.rem(me, n)]
-    for p in range(1, n):
-        total = total + dgslots[lax.rem(me - p + n, n)]
-    dg_ref[...] = total[0]
-    db_ref[...] = total[1]
-
-    for d in range(1, n):
-        for e in range(4):
+        for e in (2, 3):
             ar1(e, d).wait_send()
             ar2(e, d).wait_send()
         dg_copy(d).wait_send()
@@ -541,31 +580,30 @@
         name="block",
         out_shape=(
             jax.ShapeDtypeStruct((tokens, width), BF16), jax.ShapeDtypeStruct((tokens, width), BF16),
-            jax.ShapeDtypeStruct((own, three * width), F32), jax.ShapeDtypeStruct((own, width), F32),
+            jax.ShapeDtypeStruct((three * width, 128), F32), jax.ShapeDtypeStruct((own, width), F32),
             jax.ShapeDtypeStruct((width,), F32), jax.ShapeDtypeStruct((width,), F32)),
         in_specs=[hbm, hbm, vmem, vmem, hbm, hbm],
-        out_specs=(hbm, hbm, hbm, hbm, vmem, vmem),
+        out_specs=(hbm,) * 6,
         scratch_shapes=[
             pltpu.VMEM((tokens, width), BF16), pltpu.VMEM((tokens, width), BF16),
             pltpu.VMEM((three * width, width), BF16), pltpu.VMEM((width, width), BF16),
-            pltpu.VMEM((width, three * width), BF16),
             pltpu.VMEM((width, tokens), BF16), pltpu.VMEM((width, tokens), BF16), pltpu.VMEM((width, tokens), BF16),
             pltpu.VMEM((three * width, tokens), BF16), pltpu.VMEM((width, tokens), BF16),
             pltpu.VMEM((1, tokens), F32), pltpu.VMEM((1, tokens), F32),
             pltpu.VMEM((width, 128), F32), pltpu.VMEM((width, 128), F32),
-            pltpu.VMEM((4, gr, BLK), F32), pltpu.VMEM((4, n, hd // 2, 128), F32),
-            pltpu.VMEM((4, n, hd // 2, 128), F32), pltpu.VMEM((4, n, hd // 2, 128), F32),
+            pltpu.VMEM((2, gr, BLK), F32), pltpu.VMEM((2, n, hd // 2, 128), F32),
+            pltpu.VMEM((2, n, hd // 2, 128), F32), pltpu.VMEM((2, n, hd // 2, 128), F32),
             pltpu.VMEM((BLK, BLK), F32), pltpu.VMEM((4, gr, gr + 16), BF16), pltpu.VMEM((4, gr + 16, gr), BF16),
             pltpu.VMEM((2, width, TT), BF16),
             pltpu.VMEM((4, chips, 2, own, width), F32), pltpu.VMEM((4, chips, own, width), F32),
             pltpu.VMEM((4, 2, own // 2, width), F32), pltpu.VMEM((4, 2, own, width), F32),
-            pltpu.VMEM((width, 128), F32), pltpu.VMEM((width, 128), F32), pltpu.VMEM((n, 2, width), F32),
-            dma((3, max(steps, 3))), dma((3, max(steps, 4))),
+            pltpu.VMEM((width, 128), F32), pltpu.VMEM((n, 2, width), F32), pltpu.VMEM((width,), F32), pltpu.VMEM((width,), F32),
+            dma((3, max(steps, 3))), dma((4, max(steps, 4))),
             dma((8, n)), dma((8, n)), dma((4, chips + 6)), dma((4, chips + 6)), dma((n,)), dma((n,)),
         ],
         compiler_params=pltpu.CompilerParams(collective_id=0, has_side_effects=True, vmem_limit_bytes=67_000_000),
     )(x_tok, dy_tok, ln_gamma, ln_beta, wt, w_out)
-    return y, dx, dwqkv.reshape(own, three, heads, hd), dwo, dg, db
+    return y, dx, dwqkv[:, :own].reshape(three, heads, hd, own).transpose(3, 0, 1, 2), dwo, dg, db
 
 
 def solution(mesh):

time: 94.8 us -> 90.6 us (0.956)
  Pallas kernels: 84 us -> 81 us
  local copies, waits for them, and re-layouts: 10 us -> 8.87 us
    pallas_call x1, Pallas kernels: 84 us -> 81 us  [local_block(): pl.pallas_call(functools.partial(kernel, n, heads, hd), name='block', out...]
    pallas_call x1 -> x0, local copies, waits for them, and re-layouts: 2.55 us -> none  [local_block(): pl.pallas_call(functools.partial(kernel, n, heads, hd), name='block', out...]
    unnamed x13 -> x16, local copies, waits for them, and re-layouts: 7.49 us -> 8.87 us
where the time goes in v2:
time: 90.6 us; the launch traced here: 90.5 us
  Pallas kernels  81 us (89%)
  local copies, waits for them, and re-layouts  8.87 us (10%)
    pallas_call x1, Pallas kernels, local_block(): pl.pallas_call(functools.partial(kernel, n, heads, hd), name='block', out...  81 us
    unnamed x16, local copies, waits for them, and re-layouts  8.87 us

profile of v2, /device:TPU:113, one launch (start us, length us, event | category | flops | bytes accessed | tf_op | source)
XLA Modules:
  0.0 90.5 jit_solution(14704918605024956447)
XLA Ops:
  0.6 81.0 %block.1 = (bf16[2048,768]{1,0:T(8,128)(2,1)}, bf16[2048,768]{1,0:T(8,128)(2,1)}, f32[2304,128]{1,0:T(8,128)}, f32[96,768]{1,0:T(8,128)}, f32[768]{0:T(1024)}, /*index=5*/f32[768]{0:T(1024)}) custom-call(bf16[2048,768]{1,0:T(8,128)(2,1)} %x_hbm.1, bf16[2048,768]{1,0:T(8,128)(2,1)} %dy_hbm.1, f32[768]{0:T(1024)} %gam_ref.1, f32[768]{0:T(1024)} %bet_ref.1, ...), custom_call_target="tpu_custom_call" | custom-call | tf_op jit(solution)/shard_map/block/pallas_call | solution.py:578
  81.6 0.0 copy-start
  81.6 3.9 %copy.18 = bf16[2048,768]{1,0:T(8,128)(2,1)} copy(bf16[2048,768]{1,0:T(8,128)(2,1)} %get-tuple-element.24) | data formatting | bytes 6291456
  85.5 0.0 copy-done
  85.5 0.0 copy-start.1
  85.5 0.0 copy-start.2
  85.5 0.0 copy-start.4
  85.5 0.0 copy-start.3
  85.5 1.7 %copy.19 = bf16[2048,768]{1,0:T(8,128)(2,1)} copy(bf16[2048,768]{1,0:T(8,128)(2,1)S(1)} %copy-done) | data formatting | bytes 6291456
  87.2 0.4 copy-done.1
  87.6 1.0 %copy.20 = f32[96,3,16,48]{0,3,2,1:T(8,128)} copy(f32[96,3,16,48]{0,3,2,1:T(8,128)S(1)} %bitcast.8) | data formatting | bytes 1769472
  88.6 0.0 copy-done.2
  88.6 0.7 copy.21
  89.3 0.0 copy-done.4
  89.3 0.6 copy.22
  89.9 0.0 copy-done.3
  89.9 0.6 copy.23
Async XLA Ops:
  81.6 3.9 %copy-start = (bf16[2048,768]{1,0:T(8,128)(2,1)S(1)}, bf16[2048,768]{1,0:T(8,128)(2,1)}, u32[]{:S(2)}) copy-start(bf16[2048,768]{1,0:T(8,128)(2,1)} %get-tuple-element.25) | copy-start | bytes 9437188
  85.5 2.1 %copy-start.1 = (f32[2304,128]{1,0:T(8,128)S(1)}, f32[2304,128]{1,0:T(8,128)}, u32[]{:S(2)}) copy-start(f32[2304,128]{1,0:T(8,128)} %get-tuple-element.14) | copy-start | bytes 3538948
  85.5 3.1 %copy-start.2 = (f32[96,768]{1,0:T(8,128)S(1)}, f32[96,768]{1,0:T(8,128)}, u32[]{:S(2)}) copy-start(f32[96,768]{1,0:T(8,128)} %get-tuple-element.27) | copy-start | bytes 884740
  85.5 3.8 %copy-start.4 = (f32[768]{0:T(1024)S(1)}, f32[768]{0:T(1024)}, u32[]{:S(2)}) copy-start(f32[768]{0:T(1024)} %get-tuple-element.28) | copy-start | bytes 9220
  85.5 4.4 %copy-start.3 = (f32[768]{0:T(1024)S(1)}, f32[768]{0:T(1024)}, u32[]{:S(2)}) copy-start(f32[768]{0:T(1024)} %get-tuple-element.29) | copy-start | bytes 9220

commit v3 on v2

--- a/solution.py
+++ b/solution.py
@@ -159,13 +159,13 @@
     def ar1(e, d):
         peer = lax.rem(me + d, n)
         return pltpu.make_async_remote_copy(
-            src_ref=comp.at[e % 2, peer], dst_ref=ar_in.at[e % 2, d], send_sem=ar_send.at[2 * e, d], recv_sem=ar_recv.at[2 * e, d],
+            src_ref=comp.at[e % 2, peer], dst_ref=ar_in.at[e % 2, d], send_sem=ar_send.at[2 * (e % 2), d - 1], recv_sem=ar_recv.at[2 * (e % 2), d - 1],
             device_id={"seq": peer}, device_id_type=MESH)
 
     def ar2(e, d):
         peer = lax.rem(me + d, n)
         return pltpu.make_async_remote_copy(
-            src_ref=ar_out.at[e % 2, 0], dst_ref=ar_out.at[e % 2, d], send_sem=ar_send.at[2 * e + 1, d], recv_sem=ar_recv.at[2 * e + 1, d],
+            src_ref=ar_out.at[e % 2, 0], dst_ref=ar_out.at[e % 2, d], send_sem=ar_send.at[2 * (e % 2) + 1, d - 1], recv_sem=ar_recv.at[2 * (e % 2) + 1, d - 1],
             device_id={"seq": peer}, device_id_type=MESH)
 
     def ar_reduce(e):
@@ -419,8 +419,7 @@
         e = du * gl
         m1 = jnp.sum(e, axis=0, keepdims=True) * (1.0 / width)
         m2 = jnp.sum(p * gl, axis=0, keepdims=True) * (1.0 / width)
-        dyt = jnp.concatenate([nt(eye, dybuf[ts, BLK * b:BLK * (b + 1)]) for b in range(nb)], axis=0)
-        dxt = (dyt + rstd * (e - m1 - xhat * m2)).astype(BF16)
+        dxt = (uT[:, ts].astype(F32) + rstd * (e - m1 - xhat * m2)).astype(BF16)
         store_tokens(dybuf, t, dxt)
 
     def w_block(j):
@@ -497,6 +496,9 @@
     bb[...] = jnp.zeros_like(bb)
     for t in range(steps + 1):
         with scope(f"DU_{t}"):
+            if t > 0:
+                for b in range(nb):
+                    uT[BLK * b:BLK * (b + 1), tok(t - 1)] = nt(eye, dybuf[tok(t - 1), BLK * b:BLK * (b + 1)]).astype(BF16)
             if t < steps:
                 du_tile(t)
             if t > 0:
@@ -512,7 +514,7 @@
 
     def dg_copy(d):
         return pltpu.make_async_remote_copy(
-            src_ref=dgslots.at[0], dst_ref=dgslots.at[d], send_sem=dg_send.at[d], recv_sem=dg_recv.at[d],
+            src_ref=dgslots.at[0], dst_ref=dgslots.at[d], send_sem=dg_send.at[d - 1], recv_sem=dg_recv.at[d - 1],
             device_id={"seq": lax.rem(me + d, n)}, device_id_type=MESH)
 
     dgrow = jnp.sum(jnp.transpose(dgacc[...]), axis=0, keepdims=True)
@@ -599,7 +601,7 @@
             pltpu.VMEM((4, 2, own // 2, width), F32), pltpu.VMEM((4, 2, own, width), F32),
             pltpu.VMEM((width, 128), F32), pltpu.VMEM((n, 2, width), F32), pltpu.VMEM((width,), F32), pltpu.VMEM((width,), F32),
             dma((3, max(steps, 3))), dma((4, max(steps, 4))),
-            dma((8, n)), dma((8, n)), dma((4, chips + 6)), dma((4, chips + 6)), dma((n,)), dma((n,)),
+            dma((4, n - 1)), dma((4, n - 1)), dma((4, chips + 6)), dma((4, chips + 6)), dma((n - 1,)), dma((n - 1,)),
         ],
         compiler_params=pltpu.CompilerParams(collective_id=0, has_side_effects=True, vmem_limit_bytes=67_000_000),
     )(x_tok, dy_tok, ln_gamma, ln_beta, wt, w_out)

time: 90.6 us -> 90 us (level)
  no operation moved by 1% of the time
where the time goes in v3:
time: 90 us; the launch traced here: 89.8 us
  Pallas kernels  80.3 us (89%)
  local copies, waits for them, and re-layouts  8.87 us (10%)
    pallas_call x1, Pallas kernels, local_block(): pl.pallas_call(functools.partial(kernel, n, heads, hd), name='block', out...  80.3 us
    unnamed x16, local copies, waits for them, and re-layouts  8.87 us

profile of v3, /device:TPU:113, one launch (start us, length us, event | category | flops | bytes accessed | tf_op | source)
XLA Modules:
  0.0 89.8 jit_solution(7029410916186231322)
XLA Ops:
  0.6 80.3 %block.1 = (bf16[2048,768]{1,0:T(8,128)(2,1)}, bf16[2048,768]{1,0:T(8,128)(2,1)}, f32[2304,128]{1,0:T(8,128)}, f32[96,768]{1,0:T(8,128)}, f32[768]{0:T(1024)}, /*index=5*/f32[768]{0:T(1024)}) custom-call(bf16[2048,768]{1,0:T(8,128)(2,1)} %x_hbm.1, bf16[2048,768]{1,0:T(8,128)(2,1)} %dy_hbm.1, f32[768]{0:T(1024)} %gam_ref.1, f32[768]{0:T(1024)} %bet_ref.1, ...), custom_call_target="tpu_custom_call" | custom-call | tf_op jit(solution)/shard_map/block/pallas_call | solution.py:580
  80.9 0.0 copy-start
  81.0 3.9 %copy.18 = bf16[2048,768]{1,0:T(8,128)(2,1)} copy(bf16[2048,768]{1,0:T(8,128)(2,1)} %get-tuple-element.24) | data formatting | bytes 6291456
  84.9 0.0 copy-done
  84.9 0.0 copy-start.1
  84.9 0.0 copy-start.2
  84.9 0.0 copy-start.4
  84.9 0.0 copy-start.3
  84.9 1.7 %copy.19 = bf16[2048,768]{1,0:T(8,128)(2,1)} copy(bf16[2048,768]{1,0:T(8,128)(2,1)S(1)} %copy-done) | data formatting | bytes 6291456
  86.5 0.4 copy-done.1
  86.9 1.0 %copy.20 = f32[96,3,16,48]{0,3,2,1:T(8,128)} copy(f32[96,3,16,48]{0,3,2,1:T(8,128)S(1)} %bitcast.8) | data formatting | bytes 1769472
  87.9 0.0 copy-done.2
  87.9 0.7 copy.21
  88.6 0.0 copy-done.4
  88.6 0.6 copy.22
  89.2 0.0 copy-done.3
  89.2 0.6 copy.23
Async XLA Ops:
  80.9 3.9 %copy-start = (bf16[2048,768]{1,0:T(8,128)(2,1)S(1)}, bf16[2048,768]{1,0:T(8,128)(2,1)}, u32[]{:S(2)}) copy-start(bf16[2048,768]{1,0:T(8,128)(2,1)} %get-tuple-element.25) | copy-start | bytes 9437188
  84.9 2.1 %copy-start.1 = (f32[2304,128]{1,0:T(8,128)S(1)}, f32[2304,128]{1,0:T(8,128)}, u32[]{:S(2)}) copy-start(f32[2304,128]{1,0:T(8,128)} %get-tuple-element.14) | copy-start | bytes 3538948
  84.9 3.1 %copy-start.2 = (f32[96,768]{1,0:T(8,128)S(1)}, f32[96,768]{1,0:T(8,128)}, u32[]{:S(2)}) copy-start(f32[96,768]{1,0:T(8,128)} %get-tuple-element.27) | copy-start | bytes 884740
  84.9 3.8 %copy-start.4 = (f32[768]{0:T(1024)S(1)}, f32[768]{0:T(1024)}, u32[]{:S(2)}) copy-start(f32[768]{0:T(1024)} %get-tuple-element.28) | copy-start | bytes 9220
  84.9 4.4 %copy-start.3 = (f32[768]{0:T(1024)S(1)}, f32[768]{0:T(1024)}, u32[]{:S(2)}) copy-start(f32[768]{0:T(1024)} %get-tuple-element.29) | copy-start | bytes 9220

commit v4 on v3

--- a/solution.py
+++ b/solution.py
@@ -478,7 +478,7 @@
                 ubuf[k, BLK * j:BLK * (j + 1), BLK * i - TT * k:BLK * (i + 1) - TT * k] = nt(
                     eye, wo[BLK * i:BLK * (i + 1), BLK * j:BLK * (j + 1)]).astype(BF16)
     with scope("Y0"):
-        pl.loop(0, steps // 2)(y_tile)
+        pl.loop(0, steps // 4)(y_tile)
     with scope("ar_finish3"):
         ar_finish(3)
     with scope("C1"):
@@ -530,7 +530,7 @@
         rs_final(0)
         rs_final(1)
     with scope("Y1"):
-        pl.loop(steps // 2, steps)(y_tile)
+        pl.loop(steps // 4, steps)(y_tile)
     with scope("final2"):
         rs_final(2)
     with scope("final3"):

time: 90 us -> 89.5 us (level)
  no operation moved by 1% of the time
where the time goes in v4:
time: 89.5 us; the launch traced here: 89.4 us
  Pallas kernels  79.9 us (89%)
  local copies, waits for them, and re-layouts  8.87 us (10%)
    pallas_call x1, Pallas kernels, local_block(): pl.pallas_call(functools.partial(kernel, n, heads, hd), name='block', out...  79.9 us
    unnamed x16, local copies, waits for them, and re-layouts  8.87 us

profile of v4, /device:TPU:113, one launch (start us, length us, event | category | flops | bytes accessed | tf_op | source)
XLA Modules:
  0.0 89.4 jit_solution(5679164891307493062)
XLA Ops:
  0.6 79.9 %block.1 = (bf16[2048,768]{1,0:T(8,128)(2,1)}, bf16[2048,768]{1,0:T(8,128)(2,1)}, f32[2304,128]{1,0:T(8,128)}, f32[96,768]{1,0:T(8,128)}, f32[768]{0:T(1024)}, /*index=5*/f32[768]{0:T(1024)}) custom-call(bf16[2048,768]{1,0:T(8,128)(2,1)} %x_hbm.1, bf16[2048,768]{1,0:T(8,128)(2,1)} %dy_hbm.1, f32[768]{0:T(1024)} %gam_ref.1, f32[768]{0:T(1024)} %bet_ref.1, ...), custom_call_target="tpu_custom_call" | custom-call | tf_op jit(solution)/shard_map/block/pallas_call | solution.py:580
  80.5 0.0 copy-start
  80.5 3.9 %copy.18 = bf16[2048,768]{1,0:T(8,128)(2,1)} copy(bf16[2048,768]{1,0:T(8,128)(2,1)} %get-tuple-element.24) | data formatting | bytes 6291456
  84.4 0.0 copy-done
  84.4 0.0 copy-start.1
  84.4 0.0 copy-start.2
  84.4 0.0 copy-start.4
  84.4 0.0 copy-start.3
  84.4 1.7 %copy.19 = bf16[2048,768]{1,0:T(8,128)(2,1)} copy(bf16[2048,768]{1,0:T(8,128)(2,1)S(1)} %copy-done) | data formatting | bytes 6291456
  86.1 0.4 copy-done.1
  86.5 1.0 %copy.20 = f32[96,3,16,48]{0,3,2,1:T(8,128)} copy(f32[96,3,16,48]{0,3,2,1:T(8,128)S(1)} %bitcast.8) | data formatting | bytes 1769472
  87.5 0.0 copy-done.2
  87.5 0.7 copy.21
  88.2 0.0 copy-done.4
  88.2 0.6 copy.22
  88.8 0.0 copy-done.3
  88.8 0.6 copy.23
Async XLA Ops:
  80.5 3.9 %copy-start = (bf16[2048,768]{1,0:T(8,128)(2,1)S(1)}, bf16[2048,768]{1,0:T(8,128)(2,1)}, u32[]{:S(2)}) copy-start(bf16[2048,768]{1,0:T(8,128)(2,1)} %get-tuple-element.25) | copy-start | bytes 9437188
  84.4 2.1 %copy-start.1 = (f32[2304,128]{1,0:T(8,128)S(1)}, f32[2304,128]{1,0:T(8,128)}, u32[]{:S(2)}) copy-start(f32[2304,128]{1,0:T(8,128)} %get-tuple-element.14) | copy-start | bytes 3538948
  84.4 3.1 %copy-start.2 = (f32[96,768]{1,0:T(8,128)S(1)}, f32[96,768]{1,0:T(8,128)}, u32[]{:S(2)}) copy-start(f32[96,768]{1,0:T(8,128)} %get-tuple-element.27) | copy-start | bytes 884740
  84.4 3.8 %copy-start.4 = (f32[768]{0:T(1024)S(1)}, f32[768]{0:T(1024)}, u32[]{:S(2)}) copy-start(f32[768]{0:T(1024)} %get-tuple-element.28) | copy-start | bytes 9220
  84.4 4.4 %copy-start.3 = (f32[768]{0:T(1024)S(1)}, f32[768]{0:T(1024)}, u32[]{:S(2)}) copy-start(f32[768]{0:T(1024)} %get-tuple-element.29) | copy-start | bytes 9220
